TPU v7x, 8 devices: a whole 2x2x1 slice. The times are simulated.
8 devices in a mesh: dp: 1 (over z), sp: 8 (over y, x, core).
Axes of the slice: x: 2, y: 2, z: 1, core: 2. Of those that a mesh axis runs over, the one named last changes fastest.
Arguments:
- tokens: bfloat16 [64, 2048], P('dp')
- positions: int32 [64], P('dp')
- k_cache: bfloat16 [64, 2048, 8, 128], P('dp', 'sp')
- v_cache: bfloat16 [64, 2048, 8, 128], P('dp', 'sp')
- w_q: bfloat16 [2048, 2048], replicated
- w_k: bfloat16 [2048, 1024], replicated
- w_v: bfloat16 [2048, 1024], replicated
- w_o: bfloat16 [2048, 2048], replicated
- attn_norm: bfloat16 [2048], replicated
- q_norm: bfloat16 [128], replicated
- k_norm: bfloat16 [128], replicated
Outputs:
- output 1: bfloat16 [64, 2048], P('dp')
- output 2: bfloat16 [64, 2048, 8, 128], P('dp', 'sp')
- output 3: bfloat16 [64, 2048, 8, 128], P('dp', 'sp')
- output 4: bfloat16 [64, 2, 8, 128], P('dp')
All inputs are finite; a program needn't handle non-finite values.
Results may differ from a plain program's by a relative error of at most 0.00659406.
Values sent between devices are 32-bit elements.
A program may use at most 1 GiB of HBM per device.

v0:
```python
import jax
import jax.numpy as jnp
from jax import lax
from jax.sharding import PartitionSpec as P

NORM_EPS = 1e-6
ROPE_THETA = 1000000.0
NEG_FILL = -1e30


def rms_scale(values, gain):
    return values * lax.rsqrt(jnp.mean(values * values, axis=-1, keepdims=True) + NORM_EPS) * gain.astype(jnp.float32)


def rope_table(positions, head_dim):
    inv_freq = ROPE_THETA ** (-jnp.arange(head_dim // 2, dtype=jnp.float32) * 2.0 / head_dim)
    angles = positions.astype(jnp.float32)[:, None] * inv_freq[None, :]
    return jnp.cos(angles)[:, None, :], jnp.sin(angles)[:, None, :]


def norm_rope(proj, gain, cos_table, sin_table):
    normed = rms_scale(proj.astype(jnp.float32), gain)
    half_dim = proj.shape[-1] // 2
    first_half = normed[..., :half_dim]
    second_half = normed[..., half_dim:]
    rotated = jnp.concatenate([first_half * cos_table - second_half * sin_table, second_half * cos_table + first_half * sin_table], axis=-1)
    return rotated.astype(jnp.bfloat16)


def project_token(tokens, positions, w_q, w_k, w_v, attn_norm, q_norm, k_norm):
    seq_count = tokens.shape[0]
    head_dim = q_norm.shape[0]
    hidden = rms_scale(tokens.astype(jnp.float32), attn_norm).astype(jnp.bfloat16)
    q_proj = jnp.dot(hidden, w_q, preferred_element_type=jnp.float32).astype(jnp.bfloat16).reshape(seq_count, -1, head_dim)
    k_proj = jnp.dot(hidden, w_k, preferred_element_type=jnp.float32).astype(jnp.bfloat16).reshape(seq_count, -1, head_dim)
    v_new = jnp.dot(hidden, w_v, preferred_element_type=jnp.float32).astype(jnp.bfloat16).reshape(seq_count, -1, head_dim)
    cos_table, sin_table = rope_table(positions, head_dim)
    return norm_rope(q_proj, q_norm, cos_table, sin_table), norm_rope(k_proj, k_norm, cos_table, sin_table), v_new


def local_attention(q_rot, k_rot, v_new, positions, k_loc, v_loc, shard_start):
    seq_count, slot_count, kv_heads, head_dim = k_loc.shape
    q_per_kv = q_rot.shape[1] // kv_heads
    score_scale = head_dim ** -0.5
    slot_ids = shard_start + jnp.arange(slot_count)
    write_mask = (slot_ids[None, :] == positions[:, None])[:, :, None, None]
    k_upd = jnp.where(write_mask, k_rot[:, None], k_loc)
    v_upd = jnp.where(write_mask, v_new[:, None], v_loc)
    q_grp = q_rot.reshape(seq_count, kv_heads, q_per_kv, head_dim)
    scores = jnp.einsum('bkgd,btkd->bkgt', q_grp, k_upd, preferred_element_type=jnp.float32) * score_scale
    live_mask = (slot_ids[None, :] <= positions[:, None])[:, None, None, :]
    local_peak = jnp.max(jnp.where(live_mask, scores, NEG_FILL), axis=-1)
    weights = jnp.where(live_mask, jnp.exp(scores - local_peak[..., None]), 0.0)
    local_sum = jnp.sum(weights, axis=-1)
    local_out = jnp.einsum('bkgt,btkd->bkgd', weights.astype(jnp.bfloat16), v_upd, preferred_element_type=jnp.float32)
    return k_upd, v_upd, local_peak, local_sum, local_out


def solution(mesh):
    cache_spec = P('dp', 'sp', None, None)

    def device_step(tokens, positions, k_cache, v_cache, w_q, w_k, w_v, w_o, attn_norm, q_norm, k_norm):
        q_rot, k_rot, v_new = project_token(tokens, positions, w_q, w_k, w_v, attn_norm, q_norm, k_norm)
        head_dim = q_norm.shape[0]
        shard_start = lax.axis_index('sp') * k_cache.shape[1]
        k_upd, v_upd, local_peak, local_sum, local_out = local_attention(q_rot, k_rot, v_new, positions, k_cache, v_cache, shard_start)
        global_peak = lax.pmax(local_peak, 'sp')
        factor = jnp.exp(local_peak - global_peak)
        packed = jnp.concatenate([local_out * factor[..., None], (local_sum * factor)[..., None]], axis=-1)
        summed = lax.psum(packed, 'sp')
        attn_out = (summed[..., :head_dim] / summed[..., head_dim:]).astype(jnp.bfloat16).reshape(tokens.shape[0], -1)
        block_out = (tokens.astype(jnp.float32) + jnp.dot(attn_out, w_o, preferred_element_type=jnp.float32)).astype(jnp.bfloat16)
        return block_out, k_upd, v_upd, jnp.stack([k_rot, v_new], axis=1)

    return jax.shard_map(device_step, mesh=mesh, in_specs=(P('dp', None), P('dp'), cache_spec, cache_spec, P(), P(), P(), P(), P(), P(), P()), out_specs=(P('dp', None), cache_spec, cache_spec, P('dp', None, None, None)), check_vma=False)
```

profile of v0, /device:TPU:0, one launch (start us, length us, event | category | flops | bytes accessed | tf_op | source)
XLA Modules:
  0.0 197.7 jit_solution(2440973918174782110)
XLA Ops:
  7.2 0.0 all-reduce.2.cloned.1.call-start
  7.2 0.7 convert_element_type.66
  7.9 0.7 convert_element_type.71
  8.5 0.7 convert_element_type.67
  9.2 1.1 fusion.16
  10.3 0.7 convert_element_type.61
  11.0 0.7 broadcast_compare_fusion.1
  11.8 3.2 %fusion.15 = bf16[8,8,8,128]{3,1,2,0:T(8,128)(2,1)S(1)} fusion(bf16[2048,1024]{1,0:T(8,128)(2,1)} %param.17, bf16[64,2048]{1,0:T(8,128)(2,1)} %param.11, f32[2048]{0:T(1024)S(1)} %convert_element_type.61, f32[64]{0:T(128)S(1)} %add_rsqrt_fusion.2), kind=kOutput, calls=%fused_computation.17 | convolution fusion | flops 269025280 | bytes 4595968 | tf_op jit(solution)/shard_map/dot_general | solution.py:36
  15.0 3.2 %fusion.14 = f32[8,8,8,128]{3,1,2,0:T(8,128)S(1)} fusion(bf16[2048,1024]{1,0:T(8,128)(2,1)} %param.16, bf16[64,2048]{1,0:T(8,128)(2,1)} %param.11, f32[2048]{0:T(1024)S(1)} %convert_element_type.61, f32[64]{0:T(128)S(1)} %add_rsqrt_fusion.2), kind=kOutput, calls=%fused_computation.16 | convolution fusion | flops 269090816 | bytes 4727040 | tf_op jit(solution)/shard_map/dot_general | solution.py:35
  18.2 0.1 multiply_reduce_fusion.1
  18.4 0.1 copy.45
  18.4 0.1 copy.46
  18.5 5.1 %fusion.6 = f32[8,8,16,128]{3,1,2,0:T(8,128)S(1)} fusion(bf16[2048,2048]{1,0:T(8,128)(2,1)} %param.15, bf16[64,2048]{1,0:T(8,128)(2,1)} %param.11, f32[2048]{0:T(1024)S(1)} %convert_element_type.61, f32[64]{0:T(128)S(1)} %add_rsqrt_fusion.2), kind=kOutput, calls=%fused_computation.10 | convolution fusion | flops 537657344 | bytes 9183488 | tf_op jit(solution)/shard_map/dot_general | solution.py:34
  23.6 0.1 copy.58
  23.7 0.2 multiply_reduce_fusion
  24.0 0.2 multiply_cosine_fusion
  24.2 0.1 multiply_multiply_fusion.1
  24.3 0.2 multiply_multiply_fusion
  24.5 0.2 subtract_convert_fusion.1
  24.7 0.2 subtract_convert_fusion
  24.9 0.1 pad_maximum_fusion.2
  25.0 44.3 %broadcast_select_fusion = (bf16[64,256,8,128]{3,2,1,0:T(8,128)(2,1)}, bf16[64,256,8,128]{3,2,1,0:T(8,128)(2,1)}) fusion(bf16[64,256,8,128]{3,2,1,0:T(8,128)(2,1)} %param.14, pred[64,256]{1,0:T(8,128)(4,1)S(1)} %get-tuple-element.13, bf16[64,8,128]{2,1,0:T(8,128)(2,1)S(1)} %bitcast.36, bf16[64,256,8,128]{3,2,1,0:T(8,128)(2,1)} %param.13, ...), kind=kLoop, calls=%fused_computation.4 | loop fusion | flops 33554432 | bytes 134496256 | tf_op jit(solution)/shard_map/jit(_where)/select_n | solution.py:48
  69.4 15.0 %select_reduce_fusion = (f32[64,8,2]{2,1,0:T(8,128)S(1)}, f32[64,8,2,256]{3,2,1,0:T(2,128)S(1)}) fusion(pred[64,256]{1,0:T(8,128)(4,1)S(1)} %get-tuple-element.12, bf16[64,256,8,128]{3,2,1,0:T(8,128)(2,1)} %get-tuple-element.11, bf16[64,8,2,64]{3,2,1,0:T(2,128)(2,1)S(1)} %bitcast.40, bf16[64,8,2,64]{3,2,1,0:T(2,128)(2,1)S(1)} %bitcast.39), kind=kOutput, calls=%fused_computation.20 | convolution fusion | flops 68418560 | bytes 34885632 | tf_op jit(solution)/shard_map/bkgd,btkd->bkgt/dot_general | solution.py:50
  84.3 0.0 copy-start
  84.3 28.0 %pmax.7 = f32[64,8,2]{2,1,0:T(8,128)S(1)} all-reduce(f32[64,8,2]{2,1,0:T(8,128)S(1)} %get-tuple-element.16), channel_id=1, replica_groups=mesh['dp'=1,'sp'=8] {'sp'}, use_global_device_ids=true, to_apply=%region_4.5 | all-reduce | flops 1024 | bytes 8192 | tf_op jit(solution)/shard_map/pmax | solution.py:67
  112.3 1.4 fusion.24
  113.8 0.1 multiply_bitcast_fusion
  113.9 3.2 %copy.50 = f32[64,8,2,1]{3,2,1,0:T(2,128)S(1)} copy(f32[64,8,2,1]{2,1,0,3:T(8,128)S(1)} %get-tuple-element.4) | data formatting | bytes 8192 | tf_op jit(solution)/shard_map/broadcast_in_dim | solution.py:69
  117.1 15.0 %fusion.10 = f32[64,8,2,128]{3,2,1,0:T(2,128)S(1)} fusion(bf16[64,256,8,128]{3,2,1,0:T(8,128)(2,1)} %get-tuple-element.10, f32[64,8,2]{2,1,0:T(8,128)S(1)} %get-tuple-element.5, f32[64,8,2,256]{3,2,1,0:T(2,128)S(1)} %get-tuple-element.17, pred[64,256]{1,0:T(8,128)(4,1)S(1)} %get-tuple-element.12, f32[64,8,2]{2,1,0:T(8,128)S(1)} %get-tuple-element.16), kind=kOutput, calls=%fused_computation.12 | convolution fusion | flops 68026368 | bytes 35151872 | tf_op jit(solution)/shard_map/bkgt,btkd->bkgd/dot_general | solution.py:55
  132.1 1.6 pad_maximum_fusion
  133.7 0.0 all-reduce.2.cloned.1.call-update
  133.7 0.8 pad_maximum_fusion.1
  134.5 44.6 %all-reduce.2.cloned.1.call-done = f32[64,8,2,129]{3,2,1,0:T(2,128)} async-done(((f32[64,8,2,129]{3,2,1,0:T(2,128)}), f32[64,8,2,129]{3,2,1,0:T(2,128)}) %all-reduce.2.cloned.1.call-update) | async-done | bytes 528400 | tf_op jit(solution)/shard_map/psum | solution.py:70
  179.1 1.1 slice.29
  180.2 3.1 %copy.57 = f32[64,8,2,1]{2,1,0,3:T(8,128)S(1)} copy(f32[64,8,2,1]{3,2,1,0:T(2,128)S(1)} %slice.29) | data formatting | bytes 8192 | tf_op jit(solution)/shard_map/div | solution.py:71
  183.3 1.7 fusion.20
  185.0 0.2 reshape.191
  185.2 0.0 copy-done
  185.2 5.7 %fusion.4 = bf16[64,2048]{1,0:T(8,128)(2,1)} fusion(bf16[64,2048]{1,0:T(8,128)(2,1)S(1)} %reshape.191, bf16[2048,2048]{1,0:T(8,128)(2,1)} %param.18, bf16[64,2048]{1,0:T(8,128)(2,1)S(1)} %copy-done), kind=kOutput, calls=%fused_computation.7 | convolution fusion | flops 537264128 | bytes 9175040 | tf_op jit(solution)/shard_map/dot_general | solution.py:72
  (7 shorter events, 0.1 us)
Async XLA Ops:
  7.2 171.9 %all-reduce.2.cloned.1.call-start = ((), (), s32[]{:S(2)}) async-start(), calls=%async_computation | async-start | bytes 2097152 | tf_op jit(solution)/shard_map/psum | solution.py:70
  84.3 100.8 %copy-start = (bf16[64,2048]{1,0:T(8,128)(2,1)S(1)}, bf16[64,2048]{1,0:T(8,128)(2,1)}, u32[]{:S(2)}) copy-start(bf16[64,2048]{1,0:T(8,128)(2,1)} %param.11) | copy-start | bytes 786436
Sparse Core Ops, SparseCore 0:
  133.8 45.2 all-reduce.1
where the time goes:
time: 198 us
  other arithmetic  55.8 us (28%)
  matrix products  47.1 us (24%)
  waiting for transfers between devices  44.6 us (23%)
  blocking collectives  28 us (14%)
  between operations  14.2 us (7%)
  local copies, waits for them, and re-layouts  7.9 us (4%)
    psum x1, waiting for transfers between devices, device_step(): summed = lax.psum(packed, 'sp')  44.6 us
    select_n x1, other arithmetic, local_attention(): v_upd = jnp.where(write_mask, v_new[:, None], v_loc)  44.3 us
    pmax x1, blocking collectives, device_step(): global_peak = lax.pmax(local_peak, 'sp')  28 us
    dot_general x1, matrix products, local_attention(): jnp.einsum('bkgt,btkd->bkgd', weights.astype(jnp.bfloat16), v_upd, prefer...  15 us
    dot_general x1, matrix products, local_attention(): jnp.einsum('bkgd,btkd->bkgt', q_grp, k_upd, preferred_element_type=jnp.fl...  15 us
    dot_general x1, matrix products, device_step(): jnp.dot(attn_out, w_o, preferred_element_type=jnp.float32)  5.66 us
    dot_general x1, matrix products, project_token(): jnp.dot(hidden, w_q, preferred_element_type=jnp.float32)  5.12 us
  transfers between devices with their start and end apart: 1, of which 1 were waited for; matrix products, arithmetic and copies ran while one was open for 0% of the time, Pallas kernels for 0%

commit v1 on v0

v1 whole, which is shorter than its diff:
```python
import jax
import jax.numpy as jnp
from jax import lax
from jax.experimental import pallas as pl
from jax.experimental.pallas import tpu as pltpu
from jax.sharding import PartitionSpec as P

NORM_EPS = 1e-6
ROPE_THETA = 1000000.0
NEG_FILL = -1e30
F32 = jnp.float32
BF16 = jnp.bfloat16

SEQS = 64
WIDTH = 2048
HEADS = 16
KV = 8
DIM = 128
SLOTS = 256
ROWS = SLOTS * KV
RANKS = 8
OWN = SEQS // RANKS
PART = OWN * HEADS + 8
CHUNK = 512
RING = 16
PAIRS = RING // 2
LAG = 3
MESH = pl.DeviceIdType.MESH


def rope_tables(positions):
    inv_freq = ROPE_THETA ** (-jnp.arange(DIM // 2, dtype=F32) * 2.0 / DIM)
    angles = positions.astype(F32)[:, None] * inv_freq[None, :]
    cos, sin = jnp.cos(angles), jnp.sin(angles)
    return jnp.concatenate([cos, cos], axis=-1), jnp.concatenate([-sin, sin], axis=-1)


def attend_kernel(pos_ref, tok_ref, cos_ref, sin_ref, an_ref, qn_ref, kn_ref, wq_ref, wk_ref, wv_ref, k_ref, v_ref,
                  part_ref, new_ref, ko_ref, vo_ref,
                  wbuf, hid, q_scr, kv_scr, key, stat, kbuf, vbuf, wsem, krs, vrs, kws, vws):
    start = lax.axis_index('sp') * SLOTS

    def weight_copy(c):
        if c < 4:
            src = wq_ref.at[:, pl.ds(c * CHUNK, CHUNK)]
        elif c < 6:
            src = wk_ref.at[:, pl.ds((c - 4) * CHUNK, CHUNK)]
        else:
            src = wv_ref.at[:, pl.ds((c - 6) * CHUNK, CHUNK)]
        return pltpu.make_async_copy(src, wbuf.at[c], wsem.at[c])

    def k_read(b):
        s = lax.rem(b, RING)
        return pltpu.make_async_copy(k_ref.at[b], kbuf.at[s], krs.at[s])

    def v_read(b):
        s = lax.rem(b, RING)
        return pltpu.make_async_copy(v_ref.at[b], vbuf.at[s], vrs.at[s])

    def k_write(b):
        s = lax.rem(b, RING)
        return pltpu.make_async_copy(kbuf.at[s], ko_ref.at[b], kws.at[s])

    def v_write(b):
        s = lax.rem(b, RING)
        return pltpu.make_async_copy(vbuf.at[s], vo_ref.at[b], vws.at[s])

    for c in range(8):
        weight_copy(c).start()

    def first_reads(b, carry):
        k_read(b).start()
        v_read(b).start()
        return carry

    lax.fori_loop(0, RING, first_reads, 0)

    x = tok_ref[...].astype(F32)
    scale = lax.rsqrt(jnp.mean(x * x, axis=-1, keepdims=True) + NORM_EPS)
    hid[...] = (x * scale * an_ref[...].astype(F32)).astype(BF16)
    row = lax.broadcasted_iota(jnp.int32, (HEADS, ROWS), 0)
    col = lax.broadcasted_iota(jnp.int32, (HEADS, ROWS), 1)
    key[...] = jnp.where((col & (KV - 1)) == (row >> 1), col, 1 << 30)

    def project(c):
        return jnp.dot(hid[...], wbuf[c], preferred_element_type=F32).astype(BF16).astype(F32)

    def norm_rope(y, gain):
        y = y * lax.rsqrt(jnp.mean(y * y, axis=-1, keepdims=True) + NORM_EPS) * gain
        return (y * cos_ref[...] + pltpu.roll(y, DIM // 2, 1) * sin_ref[...]).astype(BF16).astype(F32)

    qg = qn_ref[...].astype(F32)
    kg = kn_ref[...].astype(F32)
    for c in range(8):
        weight_copy(c).wait()
        y = project(c)
        for j in range(CHUNK // DIM):
            yh = y[:, j * DIM:(j + 1) * DIM]
            if c < 4:
                q_scr[pl.ds(c * 4 + j, SEQS, stride=HEADS), :] = norm_rope(yh, qg)
            elif c < 6:
                kv_scr[pl.ds((c - 4) * 4 + j, SEQS, stride=2 * KV), :] = norm_rope(yh, kg)
            else:
                kv_scr[pl.ds(KV + (c - 6) * 4 + j, SEQS, stride=2 * KV), :] = yh
    new_ref[...] = kv_scr[...].astype(BF16)

    row16 = lax.broadcasted_iota(jnp.int32, (16, DIM), 0)
    lane16 = lax.broadcasted_iota(jnp.int32, (HEADS, DIM), 1)

    def insert(buf, s, local, new):
        slot = jnp.clip(local, 0, SLOTS - 1)
        first = jnp.where(local == slot, (slot & 1) * KV, 64)
        block = pl.ds(pl.multiple_of((slot >> 1) * 16, 16), 16)
        both = jnp.concatenate([new, new], axis=0)
        old = buf[s, block, :].astype(F32)
        hit = (row16 >= first) & (row16 < first + KV)
        buf[s, block, :] = jnp.where(hit, both, old).astype(BF16)

    def attend(b):
        s = lax.rem(b, RING)
        local = pos_ref[b] - start
        q = q_scr[pl.ds(pl.multiple_of(b * HEADS, HEADS), HEADS), :].astype(BF16)
        scores = lax.dot_general(q, kbuf[s], (((1,), (1,)), ((), ())), preferred_element_type=F32) * (DIM ** -0.5)
        live = key[...] < (local + 1) * KV
        scores = jnp.where(live, scores, NEG_FILL)
        peak = jnp.max(scores, axis=-1, keepdims=True)
        e = jnp.where(live, jnp.exp(scores - peak), 0.0)
        total = jnp.sum(e, axis=-1, keepdims=True)
        out = jnp.dot(e.astype(BF16), vbuf[s], preferred_element_type=F32)
        return out, jnp.where(lane16 == 0, peak, total)

    def group(g, carry):
        def pair(j, carry):
            i = g * (OWN // 2) + j
            b0 = 2 * i

            @pl.when(i >= LAG)
            def _():
                for d in range(2):
                    old = b0 - 2 * LAG + d
                    k_write(old).wait()
                    v_write(old).wait()

            @pl.when((i >= LAG) & (i - LAG + PAIRS < SEQS // 2))
            def _():
                for d in range(2):
                    nxt = b0 - 2 * LAG + RING + d
                    k_read(nxt).start()
                    v_read(nxt).start()

            for d in range(2):
                k_read(b0 + d).wait()
                v_read(b0 + d).wait()
            for d in range(2):
                b = b0 + d
                s = lax.rem(b, RING)
                local = pos_ref[b] - start
                base = pl.multiple_of(b * 2 * KV, 2 * KV)
                insert(kbuf, s, local, kv_scr[pl.ds(base, KV), :])
                insert(vbuf, s, local, kv_scr[pl.ds(pl.multiple_of(base + KV, KV), KV), :])
            for d in range(2):
                out, st = attend(b0 + d)
                r = pl.multiple_of((2 * j + d) * HEADS, HEADS)
                part_ref[g, pl.ds(r, HEADS), :] = out
                stat[pl.ds(r, HEADS), :] = st
            for d in range(2):
                k_write(b0 + d).start()
                v_write(b0 + d).start()
            return carry

        lax.fori_loop(0, OWN // 2, pair, 0)
        part_ref[g, pl.ds(OWN * HEADS, 8), :] = stat[...].T[0:8, :]
        return carry

    lax.fori_loop(0, RANKS, group, 0)
    for b in range(SEQS - 2 * LAG, SEQS):
        k_write(b).wait()
        v_write(b).wait()


def combine_kernel(part_ref, tok_ref, wo_ref, out_ref, wobuf, recv, mixed, own, wsem, rs_send, rs_recv, ag_send, ag_recv):
    me = lax.axis_index('sp')
    cols = WIDTH // 4

    def wo_copy(c):
        return pltpu.make_async_copy(wo_ref.at[:, pl.ds(c * cols, cols)], wobuf.at[c], wsem.at[c])

    for c in range(4):
        wo_copy(c).start()

    barrier = pltpu.get_barrier_semaphore()
    for j in range(1, RANKS):
        pl.semaphore_signal(barrier, inc=1, device_id={'sp': lax.rem(me + j, RANKS)}, device_id_type=MESH)
    pl.semaphore_wait(barrier, RANKS - 1)

    def rs_copy(j):
        dst = lax.rem(me + j, RANKS)
        return pltpu.make_async_remote_copy(
            src_ref=part_ref.at[dst], dst_ref=recv.at[RANKS - j], send_sem=rs_send.at[j], recv_sem=rs_recv.at[RANKS - j],
            device_id={'sp': dst}, device_id_type=MESH)

    for j in range(1, RANKS):
        rs_copy(j).start()
    recv[0] = part_ref[me]
    for j in range(1, RANKS):
        rs_copy(j).wait()

    rows = OWN * HEADS
    stats = [recv[s, pl.ds(rows, 8), :].T for s in range(RANKS)]
    peaks = [st[:, 0:1] for st in stats]
    peak = peaks[0]
    for s in range(1, RANKS):
        peak = jnp.maximum(peak, peaks[s])
    total = jnp.zeros((rows, 1), F32)
    acc = jnp.zeros((rows, DIM), F32)
    for s in range(RANKS):
        w = jnp.exp(peaks[s] - peak)
        total = total + w * stats[s][:, 1:2]
        acc = acc + w * recv[s, pl.ds(0, rows), :]
    mixed[...] = acc / total
    attn = jnp.concatenate([mixed[pl.ds(h, OWN, stride=HEADS), :] for h in range(HEADS)], axis=1).astype(BF16)

    x = tok_ref[pl.ds(pl.multiple_of(me * OWN, OWN), OWN), :].astype(F32)

    def ag_copy(c, j):
        dst = lax.rem(me + j, RANKS)
        block = own.at[:, pl.ds(c * cols, cols)]
        return pltpu.make_async_remote_copy(
            src_ref=block, dst_ref=out_ref.at[pl.ds(pl.multiple_of(me * OWN, OWN), OWN), pl.ds(c * cols, cols)],
            send_sem=ag_send.at[c, j], recv_sem=ag_recv.at[c, RANKS - j], device_id={'sp': dst}, device_id_type=MESH)

    for c in range(4):
        wo_copy(c).wait()
        y = jnp.dot(attn, wobuf[c], preferred_element_type=F32) + x[:, c * cols:(c + 1) * cols]
        own[:, pl.ds(c * cols, cols)] = y
        for j in range(1, RANKS):
            ag_copy(c, j).start()
    out_ref[pl.ds(pl.multiple_of(me * OWN, OWN), OWN), :] = own[...]
    for c in range(4):
        for j in range(1, RANKS):
            ag_copy(c, j).wait()


def solution(mesh):
    cache_spec = P('dp', 'sp', None, None)
    hbm = pl.BlockSpec(memory_space=pltpu.HBM)
    vmem = pl.BlockSpec(memory_space=pltpu.VMEM)
    smem = pl.BlockSpec(memory_space=pltpu.SMEM)
    sds = jax.ShapeDtypeStruct

    def device_step(tokens, positions, k_cache, v_cache, w_q, w_k, w_v, w_o, attn_norm, q_norm, k_norm):
        cos, sin = rope_tables(positions)
        flat = (SEQS, ROWS, DIM)
        part, new, k_out, v_out = pl.pallas_call(
            attend_kernel,
            out_shape=(pltpu.VMEM((RANKS, PART, DIM), F32), sds((SEQS * 2 * KV, DIM), BF16), sds(flat, BF16), sds(flat, BF16)),
            in_specs=[smem] + [vmem] * 6 + [hbm] * 5,
            out_specs=(vmem, vmem, hbm, hbm),
            scratch_shapes=[
                pltpu.VMEM((8, WIDTH, CHUNK), BF16),
                pltpu.VMEM((SEQS, WIDTH), BF16),
                pltpu.VMEM((SEQS * HEADS, DIM), F32),
                pltpu.VMEM((SEQS * 2 * KV, DIM), F32),
                pltpu.VMEM((HEADS, ROWS), jnp.int32),
                pltpu.VMEM((OWN * HEADS, DIM), F32),
                pltpu.VMEM((RING, ROWS, DIM), BF16),
                pltpu.VMEM((RING, ROWS, DIM), BF16),
                pltpu.SemaphoreType.DMA((8,)),
                pltpu.SemaphoreType.DMA((RING,)),
                pltpu.SemaphoreType.DMA((RING,)),
                pltpu.SemaphoreType.DMA((RING,)),
                pltpu.SemaphoreType.DMA((RING,)),
            ],
            compiler_params=pltpu.CompilerParams(vmem_limit_bytes=56 << 20),
        )(positions, tokens, cos, sin, attn_norm.reshape(1, WIDTH), q_norm.reshape(1, DIM), k_norm.reshape(1, DIM),
          w_q, w_k, w_v, k_cache.reshape(flat), v_cache.reshape(flat))
        gathered = pl.pallas_call(
            combine_kernel,
            out_shape=sds((SEQS, WIDTH), F32),
            in_specs=[vmem, vmem, hbm],
            out_specs=vmem,
            scratch_shapes=[
                pltpu.VMEM((4, WIDTH, WIDTH // 4), BF16),
                pltpu.VMEM((RANKS, PART, DIM), F32),
                pltpu.VMEM((OWN * HEADS, DIM), F32),
                pltpu.VMEM((OWN, WIDTH), F32),
                pltpu.SemaphoreType.DMA((4,)),
                pltpu.SemaphoreType.DMA((RANKS,)),
                pltpu.SemaphoreType.DMA((RANKS,)),
                pltpu.SemaphoreType.DMA((4, RANKS)),
                pltpu.SemaphoreType.DMA((4, RANKS)),
            ],
            compiler_params=pltpu.CompilerParams(collective_id=0, has_side_effects=True, vmem_limit_bytes=40 << 20),
        )(part, tokens, pltpu.with_memory_space_constraint(w_o, pltpu.HBM))
        return gathered.astype(BF16), k_out.reshape(k_cache.shape), v_out.reshape(v_cache.shape), new.reshape(SEQS, 2, KV, DIM)

    return jax.shard_map(device_step, mesh=mesh, in_specs=(P('dp', None), P('dp'), cache_spec, cache_spec, P(), P(), P(), P(), P(), P(), P()), out_specs=(P('dp', None), cache_spec, cache_spec, P('dp', None, None, None)), check_vma=False)
```

time: 198 us -> 77.7 us (0.39)
  Pallas kernels: 0 us -> 73.3 us
  other arithmetic: 55.8 us -> 2.3 us
  matrix products: 47.1 us -> 0 us
  waiting for transfers between devices: 44.6 us -> 0 us
  blocking collectives: 28 us -> 0 us
  between operations: 14.2 us -> 0.66 us
  local copies, waits for them, and re-layouts: 7.9 us -> 1.29 us
    pallas_call x0 -> x2, Pallas kernels: none -> 73.3 us  [the longest x1 51.8 us: device_step(): pl.pallas_call(attend_kernel, out_shape=(pltpu.VMEM((RANKS, PART, DIM), F...]
    dot_general x6 -> x0, matrix products: 47.1 us -> none  [the longest x1 15 us: local_attention(): jnp.einsum('bkgt,btkd->bkgd', weights.astype(jnp.bfloat16), v_upd, prefer...]
    psum x1 -> x0, waiting for transfers between devices: 44.6 us -> none  [device_step(): summed = lax.psum(packed, 'sp')]
    select_n x1 -> x0, other arithmetic: 44.3 us -> none  [local_attention(): v_upd = jnp.where(write_mask, v_new[:, None], v_loc)]
    pmax x1 -> x0, blocking collectives: 28 us -> none  [device_step(): global_peak = lax.pmax(local_peak, 'sp')]
    broadcast_in_dim x1 -> x0, local copies, waits for them, and re-layouts: 3.21 us -> none  [device_step(): (local_sum * factor)[..., None]]
    div x1 -> x0, local copies, waits for them, and re-layouts: 3.11 us -> none  [device_step(): summed[..., :head_dim] / summed[..., head_dim:]]
    convert_element_type x5 -> x2, other arithmetic: 4.34 us -> 1.39 us  [the longest x1 0.73 us: device_step(): gathered.astype(BF16)]
  transfers between devices with their start and end apart: 1 -> 0, of which waited for: 1 -> 0; matrix products, arithmetic and copies ran while one was open for 0% -> 0% of each run, Pallas kernels for 0% -> 0%
where the time goes in v1:
time: 77.7 us; the launch traced here: 77.5 us
  Pallas kernels  73.3 us (94%)
  other arithmetic  2.3 us (3%)
  local copies, waits for them, and re-layouts  1.29 us (2%)
    pallas_call x1, Pallas kernels, device_step(): pl.pallas_call(attend_kernel, out_shape=(pltpu.VMEM((RANKS, PART, DIM), F...  51.8 us
    pallas_call x1, Pallas kernels, device_step(): pl.pallas_call(combine_kernel, out_shape=sds((SEQS, WIDTH), F32), in_spec...  21.5 us

profile of v1, /device:TPU:0, one launch (start us, length us, event | category | flops | bytes accessed | tf_op | source)
XLA Modules:
  0.0 77.5 jit_solution(11739066241190887417)
XLA Ops:
  0.6 0.7 convert_element_type.6
  1.3 1.3 %reshape.39.an_ref = bf16[1,2048]{1,0:T(2,128)(2,1)} reshape(bf16[2048]{0:T(1024)(128)(2,1)} %param.19) | data formatting | bytes 8192 | tf_op jit(solution)/shard_map/reshape | solution.py:275
  2.6 0.2 fusion
  2.8 0.7 pad_maximum_fusion
  3.5 0.0 copy-start
  3.5 51.8 %shard_map.138 = (f32[8,136,128]{2,1,0:T(8,128)S(1)}, bf16[1024,128]{1,0:T(8,128)(2,1)}, bf16[64,2048,128]{2,1,0:T(8,128)(2,1)}, bf16[64,2048,128]{2,1,0:T(8,128)(2,1)}) custom-call(s32[64]{0:T(128)} %pos_ref.1, bf16[64,2048]{1,0:T(8,128)(2,1)} %tok_ref.3, f32[64,128]{1,0:T(8,128)} %get-tuple-element.15.cos_ref, f32[64,128]{1,0:T(8,128)} %get-tuple-element.16.sin_ref, ...), custom_call_target="tpu_custom_call" | custom-call | tf_op jit(solution)/shard_map/pallas_call | solution.py:254
  55.3 0.0 copy-done
  55.3 21.5 %shard_map.139 = f32[64,2048]{1,0:T(8,128)S(1)} custom-call(f32[8,136,128]{2,1,0:T(8,128)S(1)} %get-tuple-element.8.part_ref, bf16[64,2048]{1,0:T(8,128)(2,1)S(1)} %copy-done, bf16[2048,2048]{1,0:T(8,128)(2,1)} %wo_ref.1), custom_call_target="tpu_custom_call" | custom-call | tf_op jit(solution)/shard_map/pallas_call | solution.py:277
  76.8 0.7 convert_element_type.7
  (1 shorter events, 0.0 us)
Async XLA Ops:
  3.5 51.8 %copy-start = (bf16[64,2048]{1,0:T(8,128)(2,1)S(1)}, bf16[64,2048]{1,0:T(8,128)(2,1)}, u32[]{:S(2)}) copy-start(bf16[64,2048]{1,0:T(8,128)(2,1)} %tok_ref.3) | copy-start | bytes 786436

commit v2 on v1

v2 whole, which is shorter than its diff:
```python
import jax
import jax.numpy as jnp
import numpy as np
from jax import lax
from jax.experimental import pallas as pl
from jax.experimental.pallas import tpu as pltpu
from jax.sharding import PartitionSpec as P

NORM_EPS = 1e-6
ROPE_THETA = 1000000.0
NEG_FILL = -1e30
F32 = jnp.float32
BF16 = jnp.bfloat16
MESH = pl.DeviceIdType.MESH

SEQS = 64
WIDTH = 2048
HEADS = 16
KV = 8
DIM = 128
SLOTS = 256
ROWS = SLOTS * KV
RANKS = 8
OWN = SEQS // RANKS
EARLY = 32
LATE = SEQS - EARLY
OWN_E = EARLY // RANKS
OWN_L = LATE // RANKS
PART_E = OWN_E * HEADS + 8
PART_L = OWN_L * HEADS + 8
CHUNK = 512
RING = 16
PAIRS = RING // 2
LAG = 3
COLS = 512
CHUNKS = WIDTH // COLS


def frequencies():
    half = ROPE_THETA ** (-np.arange(DIM // 2, dtype=np.float64) * 2.0 / DIM)
    return jnp.asarray(np.concatenate([half, half])[None, :], F32)


def head_columns():
    row = lax.broadcasted_iota(jnp.int32, (HEADS, ROWS), 0)
    col = lax.broadcasted_iota(jnp.int32, (HEADS, ROWS), 1)
    return jnp.where((col & (KV - 1)) == (row >> 1), col, 1 << 30)


def insert(buf, index, local, new):
    row = lax.broadcasted_iota(jnp.int32, (2 * KV, DIM), 0)
    slot = jnp.clip(local, 0, SLOTS - 1)
    first = jnp.where(local == slot, (slot & 1) * KV, 64)
    block = pl.ds(pl.multiple_of((slot >> 1) * 2 * KV, 2 * KV), 2 * KV)
    both = jnp.concatenate([new, new], axis=0)
    old = buf[index, block, :].astype(F32)
    hit = (row >= first) & (row < first + KV)
    buf[index, block, :] = jnp.where(hit, both, old).astype(BF16)


def scores_of(q, k):
    return lax.dot_general(q, k, (((1,), (1,)), ((), ())), preferred_element_type=F32) * (DIM ** -0.5)


def stat_tile(peak, total):
    lane = lax.broadcasted_iota(jnp.int32, (HEADS, DIM), 1)
    return jnp.where(lane == 0, peak, total)


def early_kernel(pos_ref, tok_ref, freq_ref, an_ref, qn_ref, kn_ref, wq_ref, wk_ref, wv_ref, k_ref, v_ref,
                 part_ref, q_scr, kv_scr, new_ref, ko_ref, vo_ref,
                 wbuf, hid, cos_scr, sin_scr, key, stat, kbuf, vbuf, wsem, krs, vrs, kws, vws):
    start = lax.axis_index('sp') * SLOTS

    def weight_copy(c):
        if c < 4:
            src = wq_ref.at[:, pl.ds(c * CHUNK, CHUNK)]
        elif c < 6:
            src = wk_ref.at[:, pl.ds((c - 4) * CHUNK, CHUNK)]
        else:
            src = wv_ref.at[:, pl.ds((c - 6) * CHUNK, CHUNK)]
        return pltpu.make_async_copy(src, wbuf.at[c], wsem.at[c])

    def reads(b):
        s = lax.rem(b, RING)
        return (pltpu.make_async_copy(k_ref.at[b], kbuf.at[s], krs.at[s]),
                pltpu.make_async_copy(v_ref.at[b], vbuf.at[s], vrs.at[s]))

    def writes(b):
        s = lax.rem(b, RING)
        return (pltpu.make_async_copy(kbuf.at[s], ko_ref.at[b], kws.at[s]),
                pltpu.make_async_copy(vbuf.at[s], vo_ref.at[b], vws.at[s]))

    for c in range(8):
        weight_copy(c).start()

    def first_reads(b, carry):
        for copy in reads(b):
            copy.start()
        return carry

    lax.fori_loop(0, RING, first_reads, 0)

    x = tok_ref[...].astype(F32)
    scale = lax.rsqrt(jnp.mean(x * x, axis=-1, keepdims=True) + NORM_EPS)
    hid[...] = (x * scale * an_ref[...].astype(F32)[None, :]).astype(BF16)

    def fill(b, carry):
        cos_scr[pl.ds(b, 1), :] = jnp.full((1, DIM), pos_ref[b].astype(F32), F32)
        return carry

    lax.fori_loop(0, SEQS, fill, 0)
    angle = cos_scr[...] * freq_ref[...]
    lane = lax.broadcasted_iota(jnp.int32, (SEQS, DIM), 1)
    sin = jnp.sin(angle)
    cos_scr[...] = jnp.cos(angle)
    sin_scr[...] = jnp.where(lane < DIM // 2, -sin, sin)
    key[...] = head_columns()

    def norm_rope(y, gain):
        y = y * lax.rsqrt(jnp.mean(y * y, axis=-1, keepdims=True) + NORM_EPS) * gain
        return (y * cos_scr[...] + pltpu.roll(y, DIM // 2, 1) * sin_scr[...]).astype(BF16).astype(F32)

    qg = qn_ref[...].astype(F32)[None, :]
    kg = kn_ref[...].astype(F32)[None, :]
    for c in range(8):
        weight_copy(c).wait()
        y = jnp.dot(hid[...], wbuf[c], preferred_element_type=F32).astype(BF16).astype(F32)
        for j in range(CHUNK // DIM):
            yh = y[:, j * DIM:(j + 1) * DIM]
            if c < 4:
                q_scr[pl.ds(c * 4 + j, SEQS, stride=HEADS), :] = norm_rope(yh, qg)
            elif c < 6:
                kv_scr[pl.ds((c - 4) * 4 + j, SEQS, stride=2 * KV), :] = norm_rope(yh, kg)
            else:
                kv_scr[pl.ds(KV + (c - 6) * 4 + j, SEQS, stride=2 * KV), :] = yh
    new_ref[...] = kv_scr[...].astype(BF16)

    def attend(b):
        s = lax.rem(b, RING)
        local = pos_ref[b] - start
        q = q_scr[pl.ds(pl.multiple_of(b * HEADS, HEADS), HEADS), :].astype(BF16)
        scores = scores_of(q, kbuf[s])
        live = key[...] < (local + 1) * KV
        scores = jnp.where(live, scores, NEG_FILL)
        peak = jnp.max(scores, axis=-1, keepdims=True)
        e = jnp.where(live, jnp.exp(scores - peak), 0.0)
        total = jnp.sum(e, axis=-1, keepdims=True)
        out = jnp.dot(e.astype(BF16), vbuf[s], preferred_element_type=F32)
        return out, stat_tile(peak, total)

    def group(g, carry):
        def pair(j, carry):
            i = g * (OWN_E // 2) + j
            b0 = 2 * i

            @pl.when(i >= LAG)
            def _():
                for d in range(2):
                    for copy in writes(b0 - 2 * LAG + d):
                        copy.wait()

            @pl.when((i >= LAG) & (i - LAG + PAIRS < EARLY // 2))
            def _():
                for d in range(2):
                    for copy in reads(b0 - 2 * LAG + RING + d):
                        copy.start()

            for d in range(2):
                for copy in reads(b0 + d):
                    copy.wait()
            for d in range(2):
                b = b0 + d
                s = lax.rem(b, RING)
                local = pos_ref[b] - start
                base = pl.multiple_of(b * 2 * KV, 2 * KV)
                insert(kbuf, s, local, kv_scr[pl.ds(base, KV), :])
                insert(vbuf, s, local, kv_scr[pl.ds(pl.multiple_of(base + KV, KV), KV), :])
            for d in range(2):
                out, st = attend(b0 + d)
                r = pl.multiple_of((2 * j + d) * HEADS, HEADS)
                part_ref[g, pl.ds(r, HEADS), :] = out
                stat[pl.ds(r, HEADS), :] = st
            for d in range(2):
                for copy in writes(b0 + d):
                    copy.start()
            return carry

        lax.fori_loop(0, OWN_E // 2, pair, 0)
        part_ref[g, pl.ds(OWN_E * HEADS, 8), pl.ds(0, OWN_E * HEADS)] = stat[...].T[0:8, :]
        return carry

    lax.fori_loop(0, RANKS, group, 0)
    for b in range(EARLY - 2 * LAG, EARLY):
        for copy in writes(b):
            copy.wait()


def late_kernel(pos_ref, q_ref, kv_ref, early_ref, wo_ref, k_ref, v_ref,
                out_ref, keep_k, keep_v,
                wobuf, key, stat, late, recv_e, recv_l, mixed, own,
                wsem, krs, vrs, es, er, ls, lr, gs, gr):
    me = lax.axis_index('sp')
    start = me * SLOTS

    def target(j):
        return lax.rem(me + j, RANKS)

    def sequence(n):
        return EARLY + target(n // OWN_L + 1) * OWN_L + lax.rem(n, OWN_L)

    def reads(n):
        b = sequence(n)
        return (pltpu.make_async_copy(k_ref.at[b], keep_k.at[n], krs.at[n]),
                pltpu.make_async_copy(v_ref.at[b], keep_v.at[n], vrs.at[n]))

    def wo_copy(c):
        return pltpu.make_async_copy(wo_ref.at[:, pl.ds(c * COLS, COLS)], wobuf.at[c], wsem.at[c])

    def remote(src, dst, send, recv, j):
        return pltpu.make_async_remote_copy(src_ref=src, dst_ref=dst, send_sem=send, recv_sem=recv,
                                            device_id={'sp': target(j)}, device_id_type=MESH)

    def early_copy(j):
        return remote(early_ref.at[target(j)], recv_e.at[RANKS - j], es.at[j], er.at[RANKS - j], j)

    def late_copy(j):
        return remote(late.at[j], recv_l.at[RANKS - j], ls.at[j], lr.at[RANKS - j], j)

    def start_reads(n, carry):
        for copy in reads(n):
            copy.start()
        return carry

    lax.fori_loop(0, LATE, start_reads, 0)
    for c in range(CHUNKS):
        wo_copy(c).start()

    barrier = pltpu.get_barrier_semaphore()
    for j in range(1, RANKS):
        pl.semaphore_signal(barrier, inc=1, device_id={'sp': target(j)}, device_id_type=MESH)
    pl.semaphore_wait(barrier, RANKS - 1)
    for j in range(1, RANKS):
        early_copy(j).start()
    recv_e[0] = early_ref[me]
    key[...] = head_columns()

    row16 = lax.broadcasted_iota(jnp.int32, (HEADS, 2 * KV), 0)
    col16 = lax.broadcasted_iota(jnp.int32, (HEADS, 2 * KV), 1)

    def attend(n):
        b = sequence(n)
        local = pos_ref[b] - start
        base = pl.ds(pl.multiple_of(b * HEADS, HEADS), HEADS)
        q = q_ref[base, :].astype(BF16)
        kv = kv_ref[base, :].astype(BF16)
        scores = scores_of(q, keep_k[n])
        live = key[...] < local * KV
        scores = jnp.where(live, scores, NEG_FILL)
        mine = jnp.where((local >= 0) & (local < SLOTS), row16 >> 1, 64)
        fresh = jnp.where(col16 == mine, scores_of(q, kv), NEG_FILL)
        fresh = jnp.max(fresh, axis=-1, keepdims=True)
        peak = jnp.maximum(jnp.max(scores, axis=-1, keepdims=True), fresh)
        e = jnp.where(live, jnp.exp(scores - peak), 0.0)
        ef = jnp.where(col16 == mine + KV, jnp.exp(fresh - peak), 0.0)
        total = jnp.sum(e, axis=-1, keepdims=True) + jnp.sum(ef, axis=-1, keepdims=True)
        out = jnp.dot(e.astype(BF16), keep_v[n], preferred_element_type=F32)
        out = out + jnp.dot(ef.astype(BF16), kv, preferred_element_type=F32)
        return out, stat_tile(peak, total)

    def group(g, carry):
        def pair(j, carry):
            n0 = g * OWN_L + 2 * j
            for d in range(2):
                for copy in reads(n0 + d):
                    copy.wait()
            for d in range(2):
                out, st = attend(n0 + d)
                r = pl.multiple_of((2 * j + d) * HEADS, HEADS)
                late[g + 1, pl.ds(r, HEADS), :] = out
                stat[pl.ds(r, HEADS), :] = st
            return carry

        lax.fori_loop(0, OWN_L // 2, pair, 0)
        late[g + 1, pl.ds(OWN_L * HEADS, 8), pl.ds(0, OWN_L * HEADS)] = stat[...].T[0:8, :]

        @pl.when(g + 1 < RANKS)
        def _():
            late_copy(g + 1).start()

        return carry

    lax.fori_loop(0, RANKS, group, 0)
    recv_l[0] = late[RANKS]

    def combine(recv, count):
        rows = count * HEADS
        stats = [recv[s, pl.ds(rows, 8), pl.ds(0, rows)].T for s in range(RANKS)]
        peak = stats[0][:, 0:1]
        for s in range(1, RANKS):
            peak = jnp.maximum(peak, stats[s][:, 0:1])
        total = jnp.zeros((rows, 1), F32)
        acc = jnp.zeros((rows, DIM), F32)
        for s in range(RANKS):
            w = jnp.exp(stats[s][:, 0:1] - peak)
            total = total + w * stats[s][:, 1:2]
            acc = acc + w * recv[s, pl.ds(0, rows), :]
        return acc / total

    for j in range(1, RANKS):
        early_copy(j).wait()
    mixed[pl.ds(0, OWN_E * HEADS), :] = combine(recv_e, OWN_E)
    for c in range(CHUNKS):
        wo_copy(c).wait()
    for j in range(1, RANKS):
        late_copy(j).wait()
    mixed[pl.ds(OWN_E * HEADS, OWN_L * HEADS), :] = combine(recv_l, OWN_L)
    attn = jnp.concatenate([mixed[pl.ds(h, OWN, stride=HEADS), :] for h in range(HEADS)], axis=1).astype(BF16)

    def gather_copy(c, j):
        block = pl.ds(c * COLS, COLS)
        return remote(own.at[:, block], out_ref.at[me, :, block], gs.at[c, j], gr.at[c, RANKS - j], j)

    for c in range(CHUNKS):
        own[:, pl.ds(c * COLS, COLS)] = jnp.dot(attn, wobuf[c], preferred_element_type=F32)
        for j in range(1, RANKS):
            gather_copy(c, j).start()
    out_ref[me] = own[...]
    for c in range(CHUNKS):
        for j in range(1, RANKS):
            gather_copy(c, j).wait()


def store_kernel(pos_ref, tok_ref, kv_ref, rows_ref, keep_k, keep_v, ko_in, vo_in,
                 out_ref, ko_ref, vo_ref, scr, fresh_k, fresh_v, kws, vws, fks, fvs):
    me = lax.axis_index('sp')
    start = me * SLOTS

    def sequence(n):
        return EARLY + lax.rem(me + n // OWN_L + 1, RANKS) * OWN_L + lax.rem(n, OWN_L)

    def writes(n):
        b = sequence(n)
        return (pltpu.make_async_copy(keep_k.at[n], ko_ref.at[b], kws.at[n]),
                pltpu.make_async_copy(keep_v.at[n], vo_ref.at[b], vws.at[n]))

    def fresh(n):
        b = sequence(n)
        local = pos_ref[b] - start
        block = pl.ds(pl.multiple_of(jnp.clip(local, 0, SLOTS - 1) * KV, KV), KV)
        return ((local >= 0) & (local < SLOTS),
                (pltpu.make_async_copy(fresh_k.at[n], ko_ref.at[b, block], fks), pltpu.make_async_copy(fresh_v.at[n], vo_ref.at[b, block], fvs)))

    def begin(n, carry):
        for copy in writes(n):
            copy.start()
        return carry

    lax.fori_loop(0, LATE, begin, 0)

    def stage(n, carry):
        base = pl.multiple_of(sequence(n) * 2 * KV, 2 * KV)
        fresh_k[n] = kv_ref[pl.ds(base, KV), :].astype(BF16)
        fresh_v[n] = kv_ref[pl.ds(pl.multiple_of(base + KV, KV), KV), :].astype(BF16)
        return carry

    lax.fori_loop(0, LATE, stage, 0)
    for d in range(RANKS):
        scr[pl.ds(d * OWN_E, OWN_E), :] = rows_ref[d, pl.ds(0, OWN_E), :]
        scr[pl.ds(EARLY + d * OWN_L, OWN_L), :] = rows_ref[d, pl.ds(OWN_E, OWN_L), :]
    out_ref[...] = (tok_ref[...].astype(F32) + scr[...]).astype(BF16)

    def follow(n, carry):
        mine, copies = fresh(n)
        for copy in writes(n):
            copy.wait()

        @pl.when(mine)
        def _():
            for copy in copies:
                copy.start()

        return carry

    lax.fori_loop(0, LATE, follow, 0)

    def drain(n, carry):
        mine, copies = fresh(n)

        @pl.when(mine)
        def _():
            for copy in copies:
                copy.wait()

        return carry

    lax.fori_loop(0, LATE, drain, 0)


def solution(mesh):
    cache_spec = P('dp', 'sp', None, None)
    hbm = pl.BlockSpec(memory_space=pltpu.HBM)
    vmem = pl.BlockSpec(memory_space=pltpu.VMEM)
    smem = pl.BlockSpec(memory_space=pltpu.SMEM)
    sds = jax.ShapeDtypeStruct
    flat = (SEQS, ROWS, DIM)
    dma = pltpu.SemaphoreType.DMA
    space = pltpu.VMEM

    def in_vmem(a):
        return pltpu.with_memory_space_constraint(a, pltpu.VMEM)

    def in_hbm(a):
        return pltpu.with_memory_space_constraint(a, pltpu.HBM)

    def device_step(tokens, positions, k_cache, v_cache, w_q, w_k, w_v, w_o, attn_norm, q_norm, k_norm):
        k_flat, v_flat = k_cache.reshape(flat), v_cache.reshape(flat)
        early, q, kv, new, k_out, v_out = pl.pallas_call(
            early_kernel,
            out_shape=(space((RANKS, PART_E, DIM), F32), space((SEQS * HEADS, DIM), F32), space((SEQS * 2 * KV, DIM), F32),
                       sds((SEQS * 2 * KV, DIM), BF16), sds(flat, BF16), sds(flat, BF16)),
            in_specs=[smem] + [vmem] * 5 + [hbm] * 5,
            out_specs=(vmem,) * 4 + (hbm,) * 2,
            scratch_shapes=[
                space((8, WIDTH, CHUNK), BF16), space((SEQS, WIDTH), BF16), space((SEQS, DIM), F32), space((SEQS, DIM), F32),
                space((HEADS, ROWS), jnp.int32), space((OWN_E * HEADS, DIM), F32),
                space((RING, ROWS, DIM), BF16), space((RING, ROWS, DIM), BF16),
                dma((8,)), dma((RING,)), dma((RING,)), dma((RING,)), dma((RING,)),
            ],
            compiler_params=pltpu.CompilerParams(vmem_limit_bytes=58 << 20),
        )(positions, tokens, frequencies(), attn_norm, q_norm, k_norm, in_hbm(w_q), in_hbm(w_k), in_hbm(w_v), in_hbm(k_flat), in_hbm(v_flat))
        rows, keep_k, keep_v = pl.pallas_call(
            late_kernel,
            out_shape=(space((RANKS, OWN, WIDTH), F32), space((LATE, ROWS, DIM), BF16), space((LATE, ROWS, DIM), BF16)),
            in_specs=[smem] + [vmem] * 3 + [hbm] * 3,
            out_specs=(vmem,) * 3,
            scratch_shapes=[
                space((CHUNKS, WIDTH, COLS), BF16), space((HEADS, ROWS), jnp.int32), space((OWN_L * HEADS, DIM), F32),
                space((RANKS + 1, PART_L, DIM), F32), space((RANKS, PART_E, DIM), F32), space((RANKS, PART_L, DIM), F32),
                space((OWN * HEADS, DIM), F32), space((OWN, WIDTH), F32),
                dma((CHUNKS,)), dma((LATE,)), dma((LATE,)), dma((RANKS,)), dma((RANKS,)), dma((RANKS,)), dma((RANKS,)),
                dma((CHUNKS, RANKS)), dma((CHUNKS, RANKS)),
            ],
            compiler_params=pltpu.CompilerParams(collective_id=0, has_side_effects=True, vmem_limit_bytes=12 << 20),
        )(positions, in_vmem(q), in_vmem(kv), in_vmem(early), in_hbm(w_o), in_hbm(k_flat), in_hbm(v_flat))
        block_out, k_out, v_out = pl.pallas_call(
            store_kernel,
            out_shape=(sds((SEQS, WIDTH), BF16), sds(flat, BF16), sds(flat, BF16)),
            in_specs=[smem] + [vmem] * 5 + [hbm] * 2,
            out_specs=(vmem, hbm, hbm),
            scratch_shapes=[space((SEQS, WIDTH), F32), space((LATE, KV, DIM), BF16), space((LATE, KV, DIM), BF16),
                            dma((LATE,)), dma((LATE,)), dma, dma],
            input_output_aliases={6: 1, 7: 2},
            compiler_params=pltpu.CompilerParams(vmem_limit_bytes=4 << 20),
        )(positions, tokens, in_vmem(kv), in_vmem(rows), in_vmem(keep_k), in_vmem(keep_v), k_out, v_out)
        return block_out, k_out.reshape(k_cache.shape), v_out.reshape(v_cache.shape), new.reshape(SEQS, 2, KV, DIM)

    return jax.shard_map(device_step, mesh=mesh, in_specs=(P('dp', None), P('dp'), cache_spec, cache_spec, P(), P(), P(), P(), P(), P(), P()), out_specs=(P('dp', None), cache_spec, cache_spec, P('dp', None, None, None)), check_vma=False)
```

time: 77.7 us -> 74.1 us (0.954)
  other arithmetic: 2.3 us -> 0 us
  local copies, waits for them, and re-layouts: 1.29 us -> 0.01 us
    convert_element_type x2 -> x0, other arithmetic: 1.39 us -> none  [the longest x1 0.73 us: device_step(): gathered.astype(BF16)]
    reshape x1 -> x0, local copies, waits for them, and re-layouts: 1.29 us -> none  [device_step(): attn_norm.reshape(1, WIDTH)]
    pallas_call x2 -> x3, Pallas kernels: 73.3 us -> 73.3 us  [the longest x1 30.5 us: device_step(): pl.pallas_call(late_kernel, out_shape=(space((RANKS, OWN, WIDTH), F32), s...]
where the time goes in v2:
time: 74.1 us; the launch traced here: 74 us
  Pallas kernels  73.3 us (99%)
    pallas_call x1, Pallas kernels, device_step(): pl.pallas_call(late_kernel, out_shape=(space((RANKS, OWN, WIDTH), F32), s...  30.5 us
    pallas_call x1, Pallas kernels, device_step(): pl.pallas_call(early_kernel, out_shape=(space((RANKS, PART_E, DIM), F32),...  30.1 us
    pallas_call x1, Pallas kernels, device_step(): pl.pallas_call(store_kernel, out_shape=(sds((SEQS, WIDTH), BF16), sds(fla...  12.7 us

profile of v2, /device:TPU:0, one launch (start us, length us, event | category | flops | bytes accessed | tf_op | source)
XLA Modules:
  0.0 74.0 jit_solution(12244049932128116266)
XLA Ops:
  0.6 0.0 copy-start.1
  0.6 30.1 %shard_map.147 = (f32[8,72,128]{2,1,0:T(8,128)S(1)}, f32[1024,128]{1,0:T(8,128)S(1)}, f32[1024,128]{1,0:T(8,128)S(1)}, bf16[1024,128]{1,0:T(8,128)(2,1)}, bf16[6...) custom-call(s32[64]{0:T(128)} %pos_ref.5, bf16[64,2048]{1,0:T(8,128)(2,1)} %tok_ref.3, ...), custom_call_target="tpu_custom_call" | custom-call | tf_op jit(solution)/shard_map/pallas_call | solution.py:418
  30.7 0.0 copy-done.1
  30.8 0.0 copy-start
  30.8 30.5 %shard_map.148 = (f32[8,8,2048]{2,1,0:T(8,128)S(1)}, bf16[32,2048,128]{2,1,0:T(8,128)(2,1)S(1)}, bf16[32,2048,128]{2,1,0:T(8,128)(2,1)S(1)}) custom-call(s32[64]{0:T(128)S(1)} %copy-done.1, f32[1024,128]{1,0:T(8,128)S(1)} %get-tuple-element.17.q_ref, f32[1024,128]{1,0:T(8,128)S(1)} %get-tuple-element.16.kv_ref, ...), custom_call_target="tpu_custom_call" | custom-call | tf_op jit(solution)/shard_map/pallas_call | solution.py:432
  61.3 0.0 copy-done
  61.3 12.7 %shard_map.149 = (bf16[64,2048]{1,0:T(8,128)(2,1)}, bf16[64,2048,128]{2,1,0:T(8,128)(2,1)}, bf16[64,2048,128]{2,1,0:T(8,128)(2,1)}) custom-call(s32[64]{0:T(128)S(1)} %copy-done.1, bf16[64,2048]{1,0:T(8,128)(2,1)S(1)} %copy-done, f32[1024,128]{1,0:T(8,128)S(1)} %get-tuple-element.16.kv_ref, ...), custom_call_target="tpu_custom_call", output_to_operand_aliasing={{1}: (6, {}), {2}: (7, {})} | custom-call | tf_op jit(solution)/shard_map/pallas_call | solution.py:446
Async XLA Ops:
  0.6 30.1 %copy-start.1 = (s32[64]{0:T(128)S(1)}, s32[64]{0:T(128)}, u32[]{:S(2)}) copy-start(s32[64]{0:T(128)} %pos_ref.5) | copy-start | bytes 772
  30.8 30.5 %copy-start = (bf16[64,2048]{1,0:T(8,128)(2,1)S(1)}, bf16[64,2048]{1,0:T(8,128)(2,1)}, u32[]{:S(2)}) copy-start(bf16[64,2048]{1,0:T(8,128)(2,1)} %tok_ref.3) | copy-start | bytes 786436

commit v3 on v2

--- a/solution.py
+++ b/solution.py
@@ -32,6 +32,7 @@
 RING = 16
 PAIRS = RING // 2
 LAG = 3
+AHEAD = 8
 COLS = 512
 CHUNKS = WIDTH // COLS
 
@@ -196,52 +197,58 @@
             copy.wait()
 
 
+def bit(value, place):
+    if isinstance(value, int):
+        return value // place % 2
+    return lax.rem(lax.div(value, place), 2)
+
+
+def flip(index, mask):
+    return sum(lax.rem(bit(index, p) + bit(mask, p), 2) * p for p in (1, 2, 4))
+
+
+def late_sequence(me, n):
+    return EARLY + flip(me, RANKS - 1 - lax.div(n, OWN_L)) * OWN_L + lax.rem(n, OWN_L)
+
+
 def late_kernel(pos_ref, q_ref, kv_ref, early_ref, wo_ref, k_ref, v_ref,
-                out_ref, keep_k, keep_v,
-                wobuf, key, stat, late, recv_e, recv_l, mixed, own,
-                wsem, krs, vrs, es, er, ls, lr, gs, gr):
+                out_e, out_l, keep_k, keep_v,
+                wobuf, key, stat, late, recv_e, recv_l, mixed, own_e, own_l,
+                wsem, krs, vrs, es, er, ls, lr, ges, ger, gls, glr):
     me = lax.axis_index('sp')
     start = me * SLOTS
 
-    def target(j):
-        return lax.rem(me + j, RANKS)
-
-    def sequence(n):
-        return EARLY + target(n // OWN_L + 1) * OWN_L + lax.rem(n, OWN_L)
-
     def reads(n):
-        b = sequence(n)
+        b = late_sequence(me, n)
         return (pltpu.make_async_copy(k_ref.at[b], keep_k.at[n], krs.at[n]),
                 pltpu.make_async_copy(v_ref.at[b], keep_v.at[n], vrs.at[n]))
 
     def wo_copy(c):
-        return pltpu.make_async_copy(wo_ref.at[:, pl.ds(c * COLS, COLS)], wobuf.at[c], wsem.at[c])
-
-    def remote(src, dst, send, recv, j):
+        return pltpu.make_async_copy(wo_ref.at[:, pl.ds(pl.multiple_of(c * COLS, COLS), COLS)], wobuf.at[c], wsem.at[c])
+
+    def remote(src, dst, send, recv, mask):
         return pltpu.make_async_remote_copy(src_ref=src, dst_ref=dst, send_sem=send, recv_sem=recv,
-                                            device_id={'sp': target(j)}, device_id_type=MESH)
-
-    def early_copy(j):
-        return remote(early_ref.at[target(j)], recv_e.at[RANKS - j], es.at[j], er.at[RANKS - j], j)
-
-    def late_copy(j):
-        return remote(late.at[j], recv_l.at[RANKS - j], ls.at[j], lr.at[RANKS - j], j)
+                                            device_id={'sp': flip(me, mask)}, device_id_type=MESH)
+
+    def early_copy(m):
+        return remote(early_ref.at[flip(me, m)], recv_e.at[m], es.at[m], er.at[m], m)
+
+    def late_copy(m):
+        return remote(late.at[m], recv_l.at[m], ls.at[m], lr.at[m], m)
 
     def start_reads(n, carry):
         for copy in reads(n):
             copy.start()
         return carry
 
-    lax.fori_loop(0, LATE, start_reads, 0)
-    for c in range(CHUNKS):
-        wo_copy(c).start()
+    lax.fori_loop(0, AHEAD, start_reads, 0)
 
     barrier = pltpu.get_barrier_semaphore()
-    for j in range(1, RANKS):
-        pl.semaphore_signal(barrier, inc=1, device_id={'sp': target(j)}, device_id_type=MESH)
+    for m in range(1, RANKS):
+        pl.semaphore_signal(barrier, inc=1, device_id={'sp': flip(me, m)}, device_id_type=MESH)
     pl.semaphore_wait(barrier, RANKS - 1)
-    for j in range(1, RANKS):
-        early_copy(j).start()
+    for m in range(RANKS - 1, 0, -1):
+        early_copy(m).start()
     recv_e[0] = early_ref[me]
     key[...] = head_columns()
 
@@ -249,7 +256,7 @@
     col16 = lax.broadcasted_iota(jnp.int32, (HEADS, 2 * KV), 1)
 
     def attend(n):
-        b = sequence(n)
+        b = late_sequence(me, n)
         local = pos_ref[b] - start
         base = pl.ds(pl.multiple_of(b * HEADS, HEADS), HEADS)
         q = q_ref[base, :].astype(BF16)
@@ -269,29 +276,38 @@
         return out, stat_tile(peak, total)
 
     def group(g, carry):
+        m = RANKS - 1 - g
+
+        @pl.when(g < CHUNKS)
+        def _():
+            wo_copy(g).start()
+
         def pair(j, carry):
             n0 = g * OWN_L + 2 * j
+
+            @pl.when(n0 + AHEAD < LATE)
+            def _():
+                for d in range(2):
+                    start_reads(n0 + AHEAD + d, 0)
+
             for d in range(2):
                 for copy in reads(n0 + d):
                     copy.wait()
             for d in range(2):
                 out, st = attend(n0 + d)
                 r = pl.multiple_of((2 * j + d) * HEADS, HEADS)
-                late[g + 1, pl.ds(r, HEADS), :] = out
+                late[m, pl.ds(r, HEADS), :] = out
                 stat[pl.ds(r, HEADS), :] = st
             return carry
 
         lax.fori_loop(0, OWN_L // 2, pair, 0)
-        late[g + 1, pl.ds(OWN_L * HEADS, 8), pl.ds(0, OWN_L * HEADS)] = stat[...].T[0:8, :]
+        late[m, pl.ds(OWN_L * HEADS, 8), pl.ds(0, OWN_L * HEADS)] = stat[...].T[0:8, :]
 
         @pl.when(g + 1 < RANKS)
         def _():
-            late_copy(g + 1).start()
+            late_copy(m).start()
 
         return carry
-
-    lax.fori_loop(0, RANKS, group, 0)
-    recv_l[0] = late[RANKS]
 
     def combine(recv, count):
         rows = count * HEADS
@@ -305,96 +321,137 @@
             w = jnp.exp(stats[s][:, 0:1] - peak)
             total = total + w * stats[s][:, 1:2]
             acc = acc + w * recv[s, pl.ds(0, rows), :]
-        return acc / total
-
-    for j in range(1, RANKS):
-        early_copy(j).wait()
-    mixed[pl.ds(0, OWN_E * HEADS), :] = combine(recv_e, OWN_E)
+        mixed[...] = acc / total
+        return jnp.concatenate([mixed[pl.ds(h, count, stride=HEADS), :] for h in range(HEADS)], axis=1).astype(BF16)
+
+    def gather(c, own, out, gs, gr):
+        block = pl.ds(c * COLS, COLS)
+
+        def send(mask):
+            return remote(own.at[:, block], out.at[me, :, block], gs.at[c, mask], gr.at[c, me], mask)
+
+        def relay(mask):
+            src = flip(me, mask)
+            return remote(out.at[src, :, block], out.at[src, :, block], gs.at[c, mask + 1], gr.at[c, src], 1)
+
+        def arrival(mask):
+            src = flip(me, mask)
+            return remote(own.at[:, block], out.at[src, :, block], gs.at[c, mask], gr.at[c, src], mask)
+
+        def first():
+            for mask in (6, 4, 2, 1):
+                send(mask).start()
+
+        def second():
+            for mask in (2, 4, 6):
+                arrival(mask).wait_recv()
+                relay(mask).start()
+
+        def last():
+            for mask in (1, 3, 5, 7):
+                arrival(mask).wait_recv()
+            for mask in (6, 4, 2, 1):
+                send(mask).wait_send()
+            for mask in (2, 4, 6):
+                relay(mask).wait_send()
+
+        return first, second, last
+
+    def project(recv, count, own, out, gs, gr):
+        attn = combine(recv, count)
+        stages = [gather(c, own, out, gs, gr) for c in range(2)]
+        for c in range(2):
+            block = pl.ds(c * COLS, COLS)
+            own[pl.ds(0, count), block] = jnp.dot(attn, wobuf[c], preferred_element_type=F32)
+            own[pl.ds(count, count), block] = jnp.dot(attn, wobuf[c + 2], preferred_element_type=F32)
+            stages[c][0]()
+        out[me] = own[...]
+        return stages
+
+    lax.fori_loop(0, RANKS // 2, group, 0)
+    for m in range(RANKS - 1, 0, -1):
+        early_copy(m).wait()
     for c in range(CHUNKS):
         wo_copy(c).wait()
-    for j in range(1, RANKS):
-        late_copy(j).wait()
-    mixed[pl.ds(OWN_E * HEADS, OWN_L * HEADS), :] = combine(recv_l, OWN_L)
-    attn = jnp.concatenate([mixed[pl.ds(h, OWN, stride=HEADS), :] for h in range(HEADS)], axis=1).astype(BF16)
-
-    def gather_copy(c, j):
-        block = pl.ds(c * COLS, COLS)
-        return remote(own.at[:, block], out_ref.at[me, :, block], gs.at[c, j], gr.at[c, RANKS - j], j)
-
-    for c in range(CHUNKS):
-        own[:, pl.ds(c * COLS, COLS)] = jnp.dot(attn, wobuf[c], preferred_element_type=F32)
-        for j in range(1, RANKS):
-            gather_copy(c, j).start()
-    out_ref[me] = own[...]
-    for c in range(CHUNKS):
-        for j in range(1, RANKS):
-            gather_copy(c, j).wait()
-
-
-def store_kernel(pos_ref, tok_ref, kv_ref, rows_ref, keep_k, keep_v, ko_in, vo_in,
+    stages_e = project(recv_e, OWN_E, own_e, out_e, ges, ger)
+    lax.fori_loop(RANKS // 2, RANKS, group, 0)
+    for stage in stages_e:
+        stage[1]()
+    recv_l[0] = late[0]
+    for m in range(RANKS - 1, 0, -1):
+        late_copy(m).wait()
+    stages_l = project(recv_l, OWN_L, own_l, out_l, gls, glr)
+    for stage in stages_l:
+        stage[1]()
+    for stage in stages_e + stages_l:
+        stage[2]()
+
+
+def store_kernel(pos_ref, tok_ref, kv_ref, rows_e, rows_l, keep_k, keep_v, ko_in, vo_in,
                  out_ref, ko_ref, vo_ref, scr, fresh_k, fresh_v, kws, vws, fks, fvs):
     me = lax.axis_index('sp')
     start = me * SLOTS
 
-    def sequence(n):
-        return EARLY + lax.rem(me + n // OWN_L + 1, RANKS) * OWN_L + lax.rem(n, OWN_L)
-
     def writes(n):
-        b = sequence(n)
+        b = late_sequence(me, n)
         return (pltpu.make_async_copy(keep_k.at[n], ko_ref.at[b], kws.at[n]),
                 pltpu.make_async_copy(keep_v.at[n], vo_ref.at[b], vws.at[n]))
 
     def fresh(n):
-        b = sequence(n)
-        local = pos_ref[b] - start
-        block = pl.ds(pl.multiple_of(jnp.clip(local, 0, SLOTS - 1) * KV, KV), KV)
-        return ((local >= 0) & (local < SLOTS),
-                (pltpu.make_async_copy(fresh_k.at[n], ko_ref.at[b, block], fks), pltpu.make_async_copy(fresh_v.at[n], vo_ref.at[b, block], fvs)))
-
-    def begin(n, carry):
+        b = late_sequence(me, n)
+        block = pl.ds(pl.multiple_of(jnp.clip(pos_ref[b] - start, 0, SLOTS - 1) * KV, KV), KV)
+        return (pltpu.make_async_copy(fresh_k.at[n], ko_ref.at[b, block], fks), pltpu.make_async_copy(fresh_v.at[n], vo_ref.at[b, block], fvs))
+
+    def each(action, wanted):
+        def body(n, carry):
+            local = pos_ref[late_sequence(me, n)] - start
+            mine = (local >= 0) & (local < SLOTS)
+
+            @pl.when(mine if wanted else jnp.logical_not(mine))
+            def _():
+                action(n)
+
+            return carry
+
+        lax.fori_loop(0, LATE, body, 0)
+
+    def begin(n):
         for copy in writes(n):
             copy.start()
-        return carry
-
-    lax.fori_loop(0, LATE, begin, 0)
+
+    def follow(n):
+        for copy in writes(n):
+            copy.wait()
+        for copy in fresh(n):
+            copy.start()
+
+    def drain(n):
+        for copy in writes(n):
+            copy.wait()
+
+    def drain_fresh(n):
+        for copy in fresh(n):
+            copy.wait()
+
+    each(begin, True)
+    each(begin, False)
 
     def stage(n, carry):
-        base = pl.multiple_of(sequence(n) * 2 * KV, 2 * KV)
+        base = pl.multiple_of(late_sequence(me, n) * 2 * KV, 2 * KV)
         fresh_k[n] = kv_ref[pl.ds(base, KV), :].astype(BF16)
         fresh_v[n] = kv_ref[pl.ds(pl.multiple_of(base + KV, KV), KV), :].astype(BF16)
         return carry
 
     lax.fori_loop(0, LATE, stage, 0)
-    for d in range(RANKS):
-        scr[pl.ds(d * OWN_E, OWN_E), :] = rows_ref[d, pl.ds(0, OWN_E), :]
-        scr[pl.ds(EARLY + d * OWN_L, OWN_L), :] = rows_ref[d, pl.ds(OWN_E, OWN_L), :]
+    half = WIDTH // 2
+    for rows, first, count in ((rows_e, 0, OWN_E), (rows_l, EARLY, OWN_L)):
+        for d in range(RANKS):
+            scr[pl.ds(first + d * count, count), pl.ds(0, half)] = rows[d, pl.ds(0, count), :]
+            scr[pl.ds(first + d * count, count), pl.ds(half, half)] = rows[d, pl.ds(count, count), :]
     out_ref[...] = (tok_ref[...].astype(F32) + scr[...]).astype(BF16)
-
-    def follow(n, carry):
-        mine, copies = fresh(n)
-        for copy in writes(n):
-            copy.wait()
-
-        @pl.when(mine)
-        def _():
-            for copy in copies:
-                copy.start()
-
-        return carry
-
-    lax.fori_loop(0, LATE, follow, 0)
-
-    def drain(n, carry):
-        mine, copies = fresh(n)
-
-        @pl.when(mine)
-        def _():
-            for copy in copies:
-                copy.wait()
-
-        return carry
-
-    lax.fori_loop(0, LATE, drain, 0)
+    each(follow, True)
+    each(drain, False)
+    each(drain_fresh, True)
 
 
 def solution(mesh):
@@ -429,30 +486,31 @@
             ],
             compiler_params=pltpu.CompilerParams(vmem_limit_bytes=58 << 20),
         )(positions, tokens, frequencies(), attn_norm, q_norm, k_norm, in_hbm(w_q), in_hbm(w_k), in_hbm(w_v), in_hbm(k_flat), in_hbm(v_flat))
-        rows, keep_k, keep_v = pl.pallas_call(
+        rows_e, rows_l, keep_k, keep_v = pl.pallas_call(
             late_kernel,
-            out_shape=(space((RANKS, OWN, WIDTH), F32), space((LATE, ROWS, DIM), BF16), space((LATE, ROWS, DIM), BF16)),
+            out_shape=(space((RANKS, 2 * OWN_E, WIDTH // 2), F32), space((RANKS, 2 * OWN_L, WIDTH // 2), F32),
+                       space((LATE, ROWS, DIM), BF16), space((LATE, ROWS, DIM), BF16)),
             in_specs=[smem] + [vmem] * 3 + [hbm] * 3,
-            out_specs=(vmem,) * 3,
+            out_specs=(vmem,) * 4,
             scratch_shapes=[
                 space((CHUNKS, WIDTH, COLS), BF16), space((HEADS, ROWS), jnp.int32), space((OWN_L * HEADS, DIM), F32),
-                space((RANKS + 1, PART_L, DIM), F32), space((RANKS, PART_E, DIM), F32), space((RANKS, PART_L, DIM), F32),
-                space((OWN * HEADS, DIM), F32), space((OWN, WIDTH), F32),
+                space((RANKS, PART_L, DIM), F32), space((RANKS, PART_E, DIM), F32), space((RANKS, PART_L, DIM), F32),
+                space((OWN_L * HEADS, DIM), F32), space((2 * OWN_E, WIDTH // 2), F32), space((2 * OWN_L, WIDTH // 2), F32),
                 dma((CHUNKS,)), dma((LATE,)), dma((LATE,)), dma((RANKS,)), dma((RANKS,)), dma((RANKS,)), dma((RANKS,)),
-                dma((CHUNKS, RANKS)), dma((CHUNKS, RANKS)),
+                dma((2, RANKS)), dma((2, RANKS)), dma((2, RANKS)), dma((2, RANKS)),
             ],
             compiler_params=pltpu.CompilerParams(collective_id=0, has_side_effects=True, vmem_limit_bytes=12 << 20),
         )(positions, in_vmem(q), in_vmem(kv), in_vmem(early), in_hbm(w_o), in_hbm(k_flat), in_hbm(v_flat))
         block_out, k_out, v_out = pl.pallas_call(
             store_kernel,
             out_shape=(sds((SEQS, WIDTH), BF16), sds(flat, BF16), sds(flat, BF16)),
-            in_specs=[smem] + [vmem] * 5 + [hbm] * 2,
+            in_specs=[smem] + [vmem] * 6 + [hbm] * 2,
             out_specs=(vmem, hbm, hbm),
             scratch_shapes=[space((SEQS, WIDTH), F32), space((LATE, KV, DIM), BF16), space((LATE, KV, DIM), BF16),
                             dma((LATE,)), dma((LATE,)), dma, dma],
-            input_output_aliases={6: 1, 7: 2},
+            input_output_aliases={7: 1, 8: 2},
             compiler_params=pltpu.CompilerParams(vmem_limit_bytes=4 << 20),
-        )(positions, tokens, in_vmem(kv), in_vmem(rows), in_vmem(keep_k), in_vmem(keep_v), k_out, v_out)
+        )(positions, tokens, in_vmem(kv), in_vmem(rows_e), in_vmem(rows_l), in_vmem(keep_k), in_vmem(keep_v), k_out, v_out)
         return block_out, k_out.reshape(k_cache.shape), v_out.reshape(v_cache.shape), new.reshape(SEQS, 2, KV, DIM)
 
     return jax.shard_map(device_step, mesh=mesh, in_specs=(P('dp', None), P('dp'), cache_spec, cache_spec, P(), P(), P(), P(), P(), P(), P()), out_specs=(P('dp', None), cache_spec, cache_spec, P('dp', None, None, None)), check_vma=False)

time: 74.1 us -> 74.2 us (level)
    pallas_call x1, Pallas kernels: 12.7 us -> 13.8 us  [device_step(): pl.pallas_call(store_kernel, out_shape=(sds((SEQS, WIDTH), BF16), sds(fla...]
    pallas_call x1, Pallas kernels: 30.5 us -> 29.6 us  [device_step(): pl.pallas_call(late_kernel, out_shape=(space((RANKS, 2 * OWN_E, WIDTH //...]
where the time goes in v3:
time: 74.2 us; the launch traced here: 74.1 us
  Pallas kernels  73.4 us (99%)
    pallas_call x1, Pallas kernels, device_step(): pl.pallas_call(early_kernel, out_shape=(space((RANKS, PART_E, DIM), F32),...  30.1 us
    pallas_call x1, Pallas kernels, device_step(): pl.pallas_call(late_kernel, out_shape=(space((RANKS, 2 * OWN_E, WIDTH //...  29.6 us
    pallas_call x1, Pallas kernels, device_step(): pl.pallas_call(store_kernel, out_shape=(sds((SEQS, WIDTH), BF16), sds(fla...  13.8 us

profile of v3, /device:TPU:0, one launch (start us, length us, event | category | flops | bytes accessed | tf_op | source)
XLA Modules:
  0.0 74.1 jit_solution(11840916583422574391)
XLA Ops:
  0.6 0.0 copy-start.1
  0.6 30.1 %shard_map.147 = (f32[8,72,128]{2,1,0:T(8,128)S(1)}, f32[1024,128]{1,0:T(8,128)S(1)}, f32[1024,128]{1,0:T(8,128)S(1)}, bf16[1024,128]{1,0:T(8,128)(2,1)}, bf16[6...) custom-call(s32[64]{0:T(128)} %pos_ref.5, bf16[64,2048]{1,0:T(8,128)(2,1)} %tok_ref.3, ...), custom_call_target="tpu_custom_call" | custom-call | tf_op jit(solution)/shard_map/pallas_call | solution.py:475
  30.7 0.0 copy-done.1
  30.8 0.0 copy-start
  30.8 29.6 %shard_map.148 = (f32[8,8,1024]{2,1,0:T(8,128)S(1)}, f32[8,8,1024]{2,1,0:T(8,128)S(1)}, bf16[32,2048,128]{2,1,0:T(8,128)(2,1)S(1)}, bf16[32,2048,128]{2,1,0:T(8,128)(2,1)S(1)}) custom-call(s32[64]{0:T(128)S(1)} %copy-done.1, f32[1024,128]{1,0:T(8,128)S(1)} %get-tuple-element.18.q_ref, f32[1024,128]{1,0:T(8,128)S(1)} %get-tuple-element.17.kv_ref, ...), custom_call_target="tpu_custom_call" | custom-call | tf_op jit(solution)/shard_map/pallas_call | solution.py:489
  60.3 0.0 copy-done
  60.3 13.8 %shard_map.149 = (bf16[64,2048]{1,0:T(8,128)(2,1)}, bf16[64,2048,128]{2,1,0:T(8,128)(2,1)}, bf16[64,2048,128]{2,1,0:T(8,128)(2,1)}) custom-call(s32[64]{0:T(128)S(1)} %copy-done.1, bf16[64,2048]{1,0:T(8,128)(2,1)S(1)} %copy-done, f32[1024,128]{1,0:T(8,128)S(1)} %get-tuple-element.17.kv_ref, ...), custom_call_target="tpu_custom_call", output_to_operand_aliasing={{1}: (7, {}), {2}: (8, {})} | custom-call | tf_op jit(solution)/shard_map/pallas_call | solution.py:504
Async XLA Ops:
  0.6 30.1 %copy-start.1 = (s32[64]{0:T(128)S(1)}, s32[64]{0:T(128)}, u32[]{:S(2)}) copy-start(s32[64]{0:T(128)} %pos_ref.5) | copy-start | bytes 772
  30.8 29.6 %copy-start = (bf16[64,2048]{1,0:T(8,128)(2,1)S(1)}, bf16[64,2048]{1,0:T(8,128)(2,1)}, u32[]{:S(2)}) copy-start(bf16[64,2048]{1,0:T(8,128)(2,1)} %tok_ref.3) | copy-start | bytes 786436

commit v4 on v3

--- a/solution.py
+++ b/solution.py
@@ -212,8 +212,8 @@
 
 
 def late_kernel(pos_ref, q_ref, kv_ref, early_ref, wo_ref, k_ref, v_ref,
-                out_e, out_l, keep_k, keep_v,
-                wobuf, key, stat, late, recv_e, recv_l, mixed, own_e, own_l,
+                out_e, out_l, wobuf, keep_k, keep_v,
+                key, stat, late, recv_e, recv_l, own_e, own_l,
                 wsem, krs, vrs, es, er, ls, lr, ges, ger, gls, glr):
     me = lax.axis_index('sp')
     start = me * SLOTS
@@ -241,7 +241,7 @@
             copy.start()
         return carry
 
-    lax.fori_loop(0, AHEAD, start_reads, 0)
+    lax.fori_loop(0, 4, start_reads, 0)
 
     barrier = pltpu.get_barrier_semaphore()
     for m in range(1, RANKS):
@@ -249,6 +249,7 @@
     pl.semaphore_wait(barrier, RANKS - 1)
     for m in range(RANKS - 1, 0, -1):
         early_copy(m).start()
+    lax.fori_loop(4, AHEAD, start_reads, 0)
     recv_e[0] = early_ref[me]
     key[...] = head_columns()
 
@@ -278,10 +279,6 @@
     def group(g, carry):
         m = RANKS - 1 - g
 
-        @pl.when(g < CHUNKS)
-        def _():
-            wo_copy(g).start()
-
         def pair(j, carry):
             n0 = g * OWN_L + 2 * j
 
@@ -289,6 +286,11 @@
             def _():
                 for d in range(2):
                     start_reads(n0 + AHEAD + d, 0)
+
+            @pl.when(n0 + AHEAD == LATE)
+            def _():
+                for c in range(CHUNKS):
+                    wo_copy(c).start()
 
             for d in range(2):
                 for copy in reads(n0 + d):
@@ -321,26 +323,29 @@
             w = jnp.exp(stats[s][:, 0:1] - peak)
             total = total + w * stats[s][:, 1:2]
             acc = acc + w * recv[s, pl.ds(0, rows), :]
-        mixed[...] = acc / total
-        return jnp.concatenate([mixed[pl.ds(h, count, stride=HEADS), :] for h in range(HEADS)], axis=1).astype(BF16)
-
-    def gather(c, own, out, gs, gr):
-        block = pl.ds(c * COLS, COLS)
+        return acc / total
+
+    def gather(own, out, gs, gr):
+        size = own.shape[0]
+
+        def place(rank):
+            return out.at[pl.ds(pl.multiple_of(rank * size, size), size), :]
 
         def send(mask):
-            return remote(own.at[:, block], out.at[me, :, block], gs.at[c, mask], gr.at[c, me], mask)
+            return remote(own, place(me), gs.at[mask], gr.at[me], mask)
 
         def relay(mask):
             src = flip(me, mask)
-            return remote(out.at[src, :, block], out.at[src, :, block], gs.at[c, mask + 1], gr.at[c, src], 1)
+            return remote(place(src), place(src), gs.at[mask + 1], gr.at[src], 1)
 
         def arrival(mask):
             src = flip(me, mask)
-            return remote(own.at[:, block], out.at[src, :, block], gs.at[c, mask], gr.at[c, src], mask)
+            return remote(own, place(src), gs.at[mask], gr.at[src], mask)
 
         def first():
             for mask in (6, 4, 2, 1):
                 send(mask).start()
+            out[pl.ds(pl.multiple_of(me * size, size), size), :] = own[...]
 
         def second():
             for mask in (2, 4, 6):
@@ -357,101 +362,69 @@
 
         return first, second, last
 
-    def project(recv, count, own, out, gs, gr):
-        attn = combine(recv, count)
-        stages = [gather(c, own, out, gs, gr) for c in range(2)]
-        for c in range(2):
-            block = pl.ds(c * COLS, COLS)
-            own[pl.ds(0, count), block] = jnp.dot(attn, wobuf[c], preferred_element_type=F32)
-            own[pl.ds(count, count), block] = jnp.dot(attn, wobuf[c + 2], preferred_element_type=F32)
-            stages[c][0]()
-        out[me] = own[...]
-        return stages
-
-    lax.fori_loop(0, RANKS // 2, group, 0)
+    stages_e = gather(own_e, out_e, ges, ger)
+    stages_l = gather(own_l, out_l, gls, glr)
+    lax.fori_loop(0, RANKS - 1, group, 0)
     for m in range(RANKS - 1, 0, -1):
         early_copy(m).wait()
-    for c in range(CHUNKS):
-        wo_copy(c).wait()
-    stages_e = project(recv_e, OWN_E, own_e, out_e, ges, ger)
-    lax.fori_loop(RANKS // 2, RANKS, group, 0)
-    for stage in stages_e:
-        stage[1]()
+    own_e[...] = combine(recv_e, OWN_E)
+    stages_e[0]()
+    lax.fori_loop(RANKS - 1, RANKS, group, 0)
     recv_l[0] = late[0]
     for m in range(RANKS - 1, 0, -1):
         late_copy(m).wait()
-    stages_l = project(recv_l, OWN_L, own_l, out_l, gls, glr)
-    for stage in stages_l:
-        stage[1]()
-    for stage in stages_e + stages_l:
-        stage[2]()
-
-
-def store_kernel(pos_ref, tok_ref, kv_ref, rows_e, rows_l, keep_k, keep_v, ko_in, vo_in,
-                 out_ref, ko_ref, vo_ref, scr, fresh_k, fresh_v, kws, vws, fks, fvs):
+    own_l[...] = combine(recv_l, OWN_L)
+    stages_l[0]()
+    stages_e[1]()
+    stages_l[1]()
+    for c in range(CHUNKS):
+        wo_copy(c).wait()
+    stages_e[2]()
+    stages_l[2]()
+
+
+def store_kernel(pos_ref, tok_ref, kv_ref, rows_e, rows_l, wobuf, keep_k_in, keep_v_in, ko_in, vo_in,
+                 out_ref, keep_k, keep_v, ko_ref, vo_ref, attn, kws, vws):
     me = lax.axis_index('sp')
     start = me * SLOTS
 
     def writes(n):
         b = late_sequence(me, n)
-        return (pltpu.make_async_copy(keep_k.at[n], ko_ref.at[b], kws.at[n]),
-                pltpu.make_async_copy(keep_v.at[n], vo_ref.at[b], vws.at[n]))
-
-    def fresh(n):
-        b = late_sequence(me, n)
-        block = pl.ds(pl.multiple_of(jnp.clip(pos_ref[b] - start, 0, SLOTS - 1) * KV, KV), KV)
-        return (pltpu.make_async_copy(fresh_k.at[n], ko_ref.at[b, block], fks), pltpu.make_async_copy(fresh_v.at[n], vo_ref.at[b, block], fvs))
-
-    def each(action, wanted):
-        def body(n, carry):
-            local = pos_ref[late_sequence(me, n)] - start
-            mine = (local >= 0) & (local < SLOTS)
-
-            @pl.when(mine if wanted else jnp.logical_not(mine))
-            def _():
-                action(n)
-
-            return carry
-
-        lax.fori_loop(0, LATE, body, 0)
-
-    def begin(n):
-        for copy in writes(n):
-            copy.start()
-
-    def follow(n):
+        return (pltpu.make_async_copy(keep_k.at[n], ko_ref.at[b], kws), pltpu.make_async_copy(keep_v.at[n], vo_ref.at[b], vws))
+
+    def step(n, carry):
+        b = late_sequence(me, jnp.minimum(n, LATE - 1))
+        local = pos_ref[b] - start
+
+        @pl.when((n < LATE) & (local >= 0) & (local < SLOTS))
+        def _():
+            base = pl.multiple_of(b * 2 * KV, 2 * KV)
+            insert(keep_k, n, local, kv_ref[pl.ds(base, KV), :])
+            insert(keep_v, n, local, kv_ref[pl.ds(pl.multiple_of(base + KV, KV), KV), :])
+
+        @pl.when(n >= 2)
+        def _():
+            for copy in writes(n - 2):
+                copy.start()
+
+        return carry
+
+    lax.fori_loop(0, LATE + 2, step, 0)
+    for h in range(HEADS):
+        block = pl.ds(h * DIM, DIM)
+        attn[pl.ds(0, EARLY), block] = rows_e[pl.ds(h, EARLY, stride=HEADS), :].astype(BF16)
+        attn[pl.ds(EARLY, LATE), block] = rows_l[pl.ds(h, LATE, stride=HEADS), :].astype(BF16)
+    for c in range(CHUNKS):
+        block = pl.ds(c * COLS, COLS)
+        y = jnp.dot(attn[...], wobuf[c], preferred_element_type=F32)
+        out_ref[:, block] = (tok_ref[:, block].astype(F32) + y).astype(BF16)
+
+    def drain(n, carry):
         for copy in writes(n):
             copy.wait()
-        for copy in fresh(n):
-            copy.start()
-
-    def drain(n):
-        for copy in writes(n):
-            copy.wait()
-
-    def drain_fresh(n):
-        for copy in fresh(n):
-            copy.wait()
-
-    each(begin, True)
-    each(begin, False)
-
-    def stage(n, carry):
-        base = pl.multiple_of(late_sequence(me, n) * 2 * KV, 2 * KV)
-        fresh_k[n] = kv_ref[pl.ds(base, KV), :].astype(BF16)
-        fresh_v[n] = kv_ref[pl.ds(pl.multiple_of(base + KV, KV), KV), :].astype(BF16)
-        return carry
-
-    lax.fori_loop(0, LATE, stage, 0)
-    half = WIDTH // 2
-    for rows, first, count in ((rows_e, 0, OWN_E), (rows_l, EARLY, OWN_L)):
-        for d in range(RANKS):
-            scr[pl.ds(first + d * count, count), pl.ds(0, half)] = rows[d, pl.ds(0, count), :]
-            scr[pl.ds(first + d * count, count), pl.ds(half, half)] = rows[d, pl.ds(count, count), :]
-    out_ref[...] = (tok_ref[...].astype(F32) + scr[...]).astype(BF16)
-    each(follow, True)
-    each(drain, False)
-    each(drain_fresh, True)
+        return carry
+
+    lax.fori_loop(0, LATE, drain, 0)
 
 
 def solution(mesh):
@@ -486,31 +459,30 @@
             ],
             compiler_params=pltpu.CompilerParams(vmem_limit_bytes=58 << 20),
         )(positions, tokens, frequencies(), attn_norm, q_norm, k_norm, in_hbm(w_q), in_hbm(w_k), in_hbm(w_v), in_hbm(k_flat), in_hbm(v_flat))
-        rows_e, rows_l, keep_k, keep_v = pl.pallas_call(
+        rows_e, rows_l, wobuf, keep_k, keep_v = pl.pallas_call(
             late_kernel,
-            out_shape=(space((RANKS, 2 * OWN_E, WIDTH // 2), F32), space((RANKS, 2 * OWN_L, WIDTH // 2), F32),
+            out_shape=(space((EARLY * HEADS, DIM), F32), space((LATE * HEADS, DIM), F32), space((CHUNKS, WIDTH, COLS), BF16),
                        space((LATE, ROWS, DIM), BF16), space((LATE, ROWS, DIM), BF16)),
             in_specs=[smem] + [vmem] * 3 + [hbm] * 3,
-            out_specs=(vmem,) * 4,
+            out_specs=(vmem,) * 5,
             scratch_shapes=[
-                space((CHUNKS, WIDTH, COLS), BF16), space((HEADS, ROWS), jnp.int32), space((OWN_L * HEADS, DIM), F32),
+                space((HEADS, ROWS), jnp.int32), space((OWN_L * HEADS, DIM), F32),
                 space((RANKS, PART_L, DIM), F32), space((RANKS, PART_E, DIM), F32), space((RANKS, PART_L, DIM), F32),
-                space((OWN_L * HEADS, DIM), F32), space((2 * OWN_E, WIDTH // 2), F32), space((2 * OWN_L, WIDTH // 2), F32),
+                space((OWN_E * HEADS, DIM), F32), space((OWN_L * HEADS, DIM), F32),
                 dma((CHUNKS,)), dma((LATE,)), dma((LATE,)), dma((RANKS,)), dma((RANKS,)), dma((RANKS,)), dma((RANKS,)),
-                dma((2, RANKS)), dma((2, RANKS)), dma((2, RANKS)), dma((2, RANKS)),
+                dma((RANKS,)), dma((RANKS,)), dma((RANKS,)), dma((RANKS,)),
             ],
-            compiler_params=pltpu.CompilerParams(collective_id=0, has_side_effects=True, vmem_limit_bytes=12 << 20),
+            compiler_params=pltpu.CompilerParams(collective_id=0, has_side_effects=True, vmem_limit_bytes=3 << 20),
         )(positions, in_vmem(q), in_vmem(kv), in_vmem(early), in_hbm(w_o), in_hbm(k_flat), in_hbm(v_flat))
-        block_out, k_out, v_out = pl.pallas_call(
+        block_out, _, _, k_out, v_out = pl.pallas_call(
             store_kernel,
-            out_shape=(sds((SEQS, WIDTH), BF16), sds(flat, BF16), sds(flat, BF16)),
-            in_specs=[smem] + [vmem] * 6 + [hbm] * 2,
-            out_specs=(vmem, hbm, hbm),
-            scratch_shapes=[space((SEQS, WIDTH), F32), space((LATE, KV, DIM), BF16), space((LATE, KV, DIM), BF16),
-                            dma((LATE,)), dma((LATE,)), dma, dma],
-            input_output_aliases={7: 1, 8: 2},
-            compiler_params=pltpu.CompilerParams(vmem_limit_bytes=4 << 20),
-        )(positions, tokens, in_vmem(kv), in_vmem(rows_e), in_vmem(rows_l), in_vmem(keep_k), in_vmem(keep_v), k_out, v_out)
+            out_shape=(sds((SEQS, WIDTH), BF16), space((LATE, ROWS, DIM), BF16), space((LATE, ROWS, DIM), BF16), sds(flat, BF16), sds(flat, BF16)),
+            in_specs=[smem] + [vmem] * 7 + [hbm] * 2,
+            out_specs=(vmem, vmem, vmem, hbm, hbm),
+            scratch_shapes=[space((SEQS, WIDTH), BF16), dma, dma],
+            input_output_aliases={6: 1, 7: 2, 8: 3, 9: 4},
+            compiler_params=pltpu.CompilerParams(vmem_limit_bytes=3 << 20),
+        )(positions, tokens, in_vmem(kv), in_vmem(rows_e), in_vmem(rows_l), in_vmem(wobuf), in_vmem(keep_k), in_vmem(keep_v), k_out, v_out)
         return block_out, k_out.reshape(k_cache.shape), v_out.reshape(v_cache.shape), new.reshape(SEQS, 2, KV, DIM)
 
     return jax.shard_map(device_step, mesh=mesh, in_specs=(P('dp', None), P('dp'), cache_spec, cache_spec, P(), P(), P(), P(), P(), P(), P()), out_specs=(P('dp', None), cache_spec, cache_spec, P('dp', None, None, None)), check_vma=False)

time: 74.2 us -> 70.6 us (0.951)
  Pallas kernels: 73.4 us -> 69.8 us
    pallas_call x2, Pallas kernels: 43.3 us -> 39.7 us  [the longest x1 27.4 us: device_step(): pl.pallas_call(late_kernel, out_shape=(space((EARLY * HEADS, DIM), F32),...]
where the time goes in v4:
time: 70.6 us; the launch traced here: 70.5 us
  Pallas kernels  69.8 us (99%)
    pallas_call x1, Pallas kernels, device_step(): pl.pallas_call(early_kernel, out_shape=(space((RANKS, PART_E, DIM), F32),...  30.1 us
    pallas_call x1, Pallas kernels, device_step(): pl.pallas_call(late_kernel, out_shape=(space((EARLY * HEADS, DIM), F32),...  27.4 us
    pallas_call x1, Pallas kernels, device_step(): pl.pallas_call(store_kernel, out_shape=(sds((SEQS, WIDTH), BF16), space((...  12.3 us

profile of v4, /device:TPU:0, one launch (start us, length us, event | category | flops | bytes accessed | tf_op | source)
XLA Modules:
  0.0 70.5 jit_solution(2501892881726117082)
XLA Ops:
  0.6 0.0 copy-start.1
  0.6 30.1 %shard_map.147 = (f32[8,72,128]{2,1,0:T(8,128)S(1)}, f32[1024,128]{1,0:T(8,128)S(1)}, f32[1024,128]{1,0:T(8,128)S(1)}, bf16[1024,128]{1,0:T(8,128)(2,1)}, bf16[6...) custom-call(s32[64]{0:T(128)} %pos_ref.5, bf16[64,2048]{1,0:T(8,128)(2,1)} %tok_ref.3, ...), custom_call_target="tpu_custom_call" | custom-call | tf_op jit(solution)/shard_map/pallas_call | solution.py:448
  30.7 0.0 copy-done.1
  30.8 0.0 copy-start
  30.8 27.4 %shard_map.148 = (f32[512,128]{1,0:T(8,128)S(1)}, f32[512,128]{1,0:T(8,128)S(1)}, bf16[4,2048,512]{2,1,0:T(8,128)(2,1)S(1)}, bf16[32,2048,128]{2,1,0:T(8,128)(2,1)S(1)}, bf16[32,2048,128]{2,1,0:T(8,128)(2,1)S(1)}) custom-call(s32[64]{0:T(128)S(1)} %copy-done.1, f32[1024,128]{1,0:T(8,128)S(1)} %get-tuple-element.19.q_ref, ...), custom_call_target="tpu_custom_call" | custom-call | tf_op jit(solution)/shard_map/pallas_call | solution.py:462
  58.2 0.0 copy-done
  58.2 12.3 %shard_map.149 = (bf16[64,2048]{1,0:T(8,128)(2,1)}, bf16[32,2048,128]{2,1,0:T(8,128)(2,1)S(1)}, bf16[32,2048,128]{2,1,0:T(8,128)(2,1)S(1)}, bf16[64,2048,128]{2,1,0:T(8,128)(2,1)}, bf16[64,2048,128]{2,1,0:T(8,128)(2,1)}) custom-call(s32[64]{0:T(128)S(1)} %copy-done.1, ...), custom_call_target="tpu_custom_call", output_to_operand_aliasing={{1}: (6, {}), {2}: (7, {}), {3}: (8, {}), {4}: (9, {})} | custom-call | tf_op jit(solution)/shard_map/pallas_call | solution.py:477
Async XLA Ops:
  0.6 30.1 %copy-start.1 = (s32[64]{0:T(128)S(1)}, s32[64]{0:T(128)}, u32[]{:S(2)}) copy-start(s32[64]{0:T(128)} %pos_ref.5) | copy-start | bytes 772
  30.8 27.4 %copy-start = (bf16[64,2048]{1,0:T(8,128)(2,1)S(1)}, bf16[64,2048]{1,0:T(8,128)(2,1)}, u32[]{:S(2)}) copy-start(bf16[64,2048]{1,0:T(8,128)(2,1)} %tok_ref.3) | copy-start | bytes 786436

commit v5 on v4

--- a/solution.py
+++ b/solution.py
@@ -22,7 +22,7 @@
 ROWS = SLOTS * KV
 RANKS = 8
 OWN = SEQS // RANKS
-EARLY = 32
+EARLY = 48
 LATE = SEQS - EARLY
 OWN_E = EARLY // RANKS
 OWN_L = LATE // RANKS

time: 70.6 us -> 67.4 us (0.955)
  Pallas kernels: 69.8 us -> 66.6 us
    pallas_call x1, Pallas kernels: 30.1 us -> 40.5 us  [device_step(): pl.pallas_call(early_kernel, out_shape=(space((RANKS, PART_E, DIM), F32),...]
    pallas_call x1, Pallas kernels: 27.4 us -> 18.9 us  [device_step(): pl.pallas_call(late_kernel, out_shape=(space((EARLY * HEADS, DIM), F32),...]
    pallas_call x1, Pallas kernels: 12.3 us -> 7.24 us  [device_step(): pl.pallas_call(store_kernel, out_shape=(sds((SEQS, WIDTH), BF16), space((...]
where the time goes in v5:
time: 67.4 us; the launch traced here: 67.3 us
  Pallas kernels  66.6 us (99%)
  between operations  0.68 us (1%)
    pallas_call x1, Pallas kernels, device_step(): pl.pallas_call(early_kernel, out_shape=(space((RANKS, PART_E, DIM), F32),...  40.5 us
    pallas_call x1, Pallas kernels, device_step(): pl.pallas_call(late_kernel, out_shape=(space((EARLY * HEADS, DIM), F32),...  18.9 us
    pallas_call x1, Pallas kernels, device_step(): pl.pallas_call(store_kernel, out_shape=(sds((SEQS, WIDTH), BF16), space((...  7.24 us

profile of v5, /device:TPU:0, one launch (start us, length us, event | category | flops | bytes accessed | tf_op | source)
XLA Modules:
  0.0 67.3 jit_solution(2604452700643571786)
XLA Ops:
  0.6 0.0 copy-start.1
  0.6 40.5 %shard_map.147 = (f32[8,104,128]{2,1,0:T(8,128)S(1)}, f32[1024,128]{1,0:T(8,128)S(1)}, f32[1024,128]{1,0:T(8,128)S(1)}, bf16[1024,128]{1,0:T(8,128)(2,1)}, bf16[...) custom-call(s32[64]{0:T(128)} %pos_ref.5, bf16[64,2048]{1,0:T(8,128)(2,1)} %tok_ref.3, ...), custom_call_target="tpu_custom_call" | custom-call | tf_op jit(solution)/shard_map/pallas_call | solution.py:448
  41.1 0.0 copy-done.1
  41.1 0.0 copy-start
  41.1 18.9 %shard_map.148 = (f32[768,128]{1,0:T(8,128)S(1)}, f32[256,128]{1,0:T(8,128)S(1)}, bf16[4,2048,512]{2,1,0:T(8,128)(2,1)S(1)}, bf16[16,2048,128]{2,1,0:T(8,128)(2,1)S(1)}, bf16[16,2048,128]{2,1,0:T(8,128)(2,1)S(1)}) custom-call(s32[64]{0:T(128)S(1)} %copy-done.1, f32[1024,128]{1,0:T(8,128)S(1)} %get-tuple-element.19.q_ref, ...), custom_call_target="tpu_custom_call" | custom-call | tf_op jit(solution)/shard_map/pallas_call | solution.py:462
  60.1 0.0 copy-done
  60.1 7.2 %shard_map.149 = (bf16[64,2048]{1,0:T(8,128)(2,1)}, bf16[16,2048,128]{2,1,0:T(8,128)(2,1)S(1)}, bf16[16,2048,128]{2,1,0:T(8,128)(2,1)S(1)}, bf16[64,2048,128]{2,1,0:T(8,128)(2,1)}, bf16[64,2048,128]{2,1,0:T(8,128)(2,1)}) custom-call(s32[64]{0:T(128)S(1)} %copy-done.1, ...), custom_call_target="tpu_custom_call", output_to_operand_aliasing={{1}: (6, {}), {2}: (7, {}), {3}: (8, {}), {4}: (9, {})} | custom-call | tf_op jit(solution)/shard_map/pallas_call | solution.py:477
Async XLA Ops:
  0.6 40.5 %copy-start.1 = (s32[64]{0:T(128)S(1)}, s32[64]{0:T(128)}, u32[]{:S(2)}) copy-start(s32[64]{0:T(128)} %pos_ref.5) | copy-start | bytes 772
  41.1 19.0 %copy-start = (bf16[64,2048]{1,0:T(8,128)(2,1)S(1)}, bf16[64,2048]{1,0:T(8,128)(2,1)}, u32[]{:S(2)}) copy-start(bf16[64,2048]{1,0:T(8,128)(2,1)} %tok_ref.3) | copy-start | bytes 786436

commit v6 on v5

--- a/solution.py
+++ b/solution.py
@@ -32,7 +32,6 @@
 RING = 16
 PAIRS = RING // 2
 LAG = 3
-AHEAD = 8
 COLS = 512
 CHUNKS = WIDTH // COLS
 
@@ -82,25 +81,28 @@
             src = wv_ref.at[:, pl.ds((c - 6) * CHUNK, CHUNK)]
         return pltpu.make_async_copy(src, wbuf.at[c], wsem.at[c])
 
-    def reads(b):
-        s = lax.rem(b, RING)
-        return (pltpu.make_async_copy(k_ref.at[b], kbuf.at[s], krs.at[s]),
-                pltpu.make_async_copy(v_ref.at[b], vbuf.at[s], vrs.at[s]))
-
-    def writes(b):
-        s = lax.rem(b, RING)
-        return (pltpu.make_async_copy(kbuf.at[s], ko_ref.at[b], kws.at[s]),
-                pltpu.make_async_copy(vbuf.at[s], vo_ref.at[b], vws.at[s]))
+    def pair_slots(i):
+        return pl.ds(2 * lax.rem(i, PAIRS), 2)
+
+    def reads(i):
+        s = lax.rem(i, PAIRS)
+        return (pltpu.make_async_copy(k_ref.at[pl.ds(2 * i, 2)], kbuf.at[pair_slots(i)], krs.at[s]),
+                pltpu.make_async_copy(v_ref.at[pl.ds(2 * i, 2)], vbuf.at[pair_slots(i)], vrs.at[s]))
+
+    def writes(i):
+        s = lax.rem(i, PAIRS)
+        return (pltpu.make_async_copy(kbuf.at[pair_slots(i)], ko_ref.at[pl.ds(2 * i, 2)], kws.at[s]),
+                pltpu.make_async_copy(vbuf.at[pair_slots(i)], vo_ref.at[pl.ds(2 * i, 2)], vws.at[s]))
 
     for c in range(8):
         weight_copy(c).start()
 
-    def first_reads(b, carry):
-        for copy in reads(b):
+    def first_reads(i, carry):
+        for copy in reads(i):
             copy.start()
         return carry
 
-    lax.fori_loop(0, RING, first_reads, 0)
+    lax.fori_loop(0, PAIRS, first_reads, 0)
 
     x = tok_ref[...].astype(F32)
     scale = lax.rsqrt(jnp.mean(x * x, axis=-1, keepdims=True) + NORM_EPS)
@@ -157,19 +159,16 @@
 
             @pl.when(i >= LAG)
             def _():
-                for d in range(2):
-                    for copy in writes(b0 - 2 * LAG + d):
-                        copy.wait()
+                for copy in writes(i - LAG):
+                    copy.wait()
 
             @pl.when((i >= LAG) & (i - LAG + PAIRS < EARLY // 2))
             def _():
-                for d in range(2):
-                    for copy in reads(b0 - 2 * LAG + RING + d):
-                        copy.start()
-
-            for d in range(2):
-                for copy in reads(b0 + d):
-                    copy.wait()
+                for copy in reads(i - LAG + PAIRS):
+                    copy.start()
+
+            for copy in reads(i):
+                copy.wait()
             for d in range(2):
                 b = b0 + d
                 s = lax.rem(b, RING)
@@ -182,9 +181,8 @@
                 r = pl.multiple_of((2 * j + d) * HEADS, HEADS)
                 part_ref[g, pl.ds(r, HEADS), :] = out
                 stat[pl.ds(r, HEADS), :] = st
-            for d in range(2):
-                for copy in writes(b0 + d):
-                    copy.start()
+            for copy in writes(i):
+                copy.start()
             return carry
 
         lax.fori_loop(0, OWN_E // 2, pair, 0)
@@ -192,8 +190,8 @@
         return carry
 
     lax.fori_loop(0, RANKS, group, 0)
-    for b in range(EARLY - 2 * LAG, EARLY):
-        for copy in writes(b):
+    for i in range(EARLY // 2 - LAG, EARLY // 2):
+        for copy in writes(i):
             copy.wait()
 
 
@@ -218,10 +216,10 @@
     me = lax.axis_index('sp')
     start = me * SLOTS
 
-    def reads(n):
-        b = late_sequence(me, n)
-        return (pltpu.make_async_copy(k_ref.at[b], keep_k.at[n], krs.at[n]),
-                pltpu.make_async_copy(v_ref.at[b], keep_v.at[n], vrs.at[n]))
+    def reads(i):
+        b = late_sequence(me, 2 * i)
+        return (pltpu.make_async_copy(k_ref.at[pl.ds(b, 2)], keep_k.at[pl.ds(2 * i, 2)], krs.at[i]),
+                pltpu.make_async_copy(v_ref.at[pl.ds(b, 2)], keep_v.at[pl.ds(2 * i, 2)], vrs.at[i]))
 
     def wo_copy(c):
         return pltpu.make_async_copy(wo_ref.at[:, pl.ds(pl.multiple_of(c * COLS, COLS), COLS)], wobuf.at[c], wsem.at[c])
@@ -241,7 +239,7 @@
             copy.start()
         return carry
 
-    lax.fori_loop(0, 4, start_reads, 0)
+    lax.fori_loop(0, 2, start_reads, 0)
 
     barrier = pltpu.get_barrier_semaphore()
     for m in range(1, RANKS):
@@ -249,7 +247,9 @@
     pl.semaphore_wait(barrier, RANKS - 1)
     for m in range(RANKS - 1, 0, -1):
         early_copy(m).start()
-    lax.fori_loop(4, AHEAD, start_reads, 0)
+    lax.fori_loop(2, LATE // 2, start_reads, 0)
+    for c in range(CHUNKS):
+        wo_copy(c).start()
     recv_e[0] = early_ref[me]
     key[...] = head_columns()
 
@@ -282,19 +282,8 @@
         def pair(j, carry):
             n0 = g * OWN_L + 2 * j
 
-            @pl.when(n0 + AHEAD < LATE)
-            def _():
-                for d in range(2):
-                    start_reads(n0 + AHEAD + d, 0)
-
-            @pl.when(n0 + AHEAD == LATE)
-            def _():
-                for c in range(CHUNKS):
-                    wo_copy(c).start()
-
-            for d in range(2):
-                for copy in reads(n0 + d):
-                    copy.wait()
+            for copy in reads(g * (OWN_L // 2) + j):
+                copy.wait()
             for d in range(2):
                 out, st = attend(n0 + d)
                 r = pl.multiple_of((2 * j + d) * HEADS, HEADS)
@@ -388,9 +377,10 @@
     me = lax.axis_index('sp')
     start = me * SLOTS
 
-    def writes(n):
-        b = late_sequence(me, n)
-        return (pltpu.make_async_copy(keep_k.at[n], ko_ref.at[b], kws), pltpu.make_async_copy(keep_v.at[n], vo_ref.at[b], vws))
+    def writes(i):
+        b = late_sequence(me, 2 * i)
+        return (pltpu.make_async_copy(keep_k.at[pl.ds(2 * i, 2)], ko_ref.at[pl.ds(b, 2)], kws),
+                pltpu.make_async_copy(keep_v.at[pl.ds(2 * i, 2)], vo_ref.at[pl.ds(b, 2)], vws))
 
     def step(n, carry):
         b = late_sequence(me, jnp.minimum(n, LATE - 1))
@@ -402,9 +392,9 @@
             insert(keep_k, n, local, kv_ref[pl.ds(base, KV), :])
             insert(keep_v, n, local, kv_ref[pl.ds(pl.multiple_of(base + KV, KV), KV), :])
 
-        @pl.when(n >= 2)
+        @pl.when((n >= 3) & (lax.rem(n, 2) == 1))
         def _():
-            for copy in writes(n - 2):
+            for copy in writes(lax.div(n - 3, 2)):
                 copy.start()
 
         return carry
@@ -424,7 +414,7 @@
             copy.wait()
         return carry
 
-    lax.fori_loop(0, LATE, drain, 0)
+    lax.fori_loop(0, LATE // 2, drain, 0)
 
 
 def solution(mesh):
@@ -455,7 +445,7 @@
                 space((8, WIDTH, CHUNK), BF16), space((SEQS, WIDTH), BF16), space((SEQS, DIM), F32), space((SEQS, DIM), F32),
                 space((HEADS, ROWS), jnp.int32), space((OWN_E * HEADS, DIM), F32),
                 space((RING, ROWS, DIM), BF16), space((RING, ROWS, DIM), BF16),
-                dma((8,)), dma((RING,)), dma((RING,)), dma((RING,)), dma((RING,)),
+                dma((8,)), dma((PAIRS,)), dma((PAIRS,)), dma((PAIRS,)), dma((PAIRS,)),
             ],
             compiler_params=pltpu.CompilerParams(vmem_limit_bytes=58 << 20),
         )(positions, tokens, frequencies(), attn_norm, q_norm, k_norm, in_hbm(w_q), in_hbm(w_k), in_hbm(w_v), in_hbm(k_flat), in_hbm(v_flat))
@@ -469,7 +459,7 @@
                 space((HEADS, ROWS), jnp.int32), space((OWN_L * HEADS, DIM), F32),
                 space((RANKS, PART_L, DIM), F32), space((RANKS, PART_E, DIM), F32), space((RANKS, PART_L, DIM), F32),
                 space((OWN_E * HEADS, DIM), F32), space((OWN_L * HEADS, DIM), F32),
-                dma((CHUNKS,)), dma((LATE,)), dma((LATE,)), dma((RANKS,)), dma((RANKS,)), dma((RANKS,)), dma((RANKS,)),
+                dma((CHUNKS,)), dma((LATE // 2,)), dma((LATE // 2,)), dma((RANKS,)), dma((RANKS,)), dma((RANKS,)), dma((RANKS,)),
                 dma((RANKS,)), dma((RANKS,)), dma((RANKS,)), dma((RANKS,)),
             ],
             compiler_params=pltpu.CompilerParams(collective_id=0, has_side_effects=True, vmem_limit_bytes=3 << 20),

time: 67.4 us -> 66.8 us (level)
  no operation moved by 1% of the time
where the time goes in v6:
time: 66.8 us; the launch traced here: 66.7 us
  Pallas kernels  66 us (99%)
  between operations  0.68 us (1%)
    pallas_call x1, Pallas kernels, device_step(): pl.pallas_call(early_kernel, out_shape=(space((RANKS, PART_E, DIM), F32),...  40.2 us
    pallas_call x1, Pallas kernels, device_step(): pl.pallas_call(late_kernel, out_shape=(space((EARLY * HEADS, DIM), F32),...  18.5 us
    pallas_call x1, Pallas kernels, device_step(): pl.pallas_call(store_kernel, out_shape=(sds((SEQS, WIDTH), BF16), space((...  7.34 us

profile of v6, /device:TPU:0, one launch (start us, length us, event | category | flops | bytes accessed | tf_op | source)
XLA Modules:
  0.0 66.7 jit_solution(2035259539851041526)
XLA Ops:
  0.6 0.0 copy-start.1
  0.6 40.2 %shard_map.147 = (f32[8,104,128]{2,1,0:T(8,128)S(1)}, f32[1024,128]{1,0:T(8,128)S(1)}, f32[1024,128]{1,0:T(8,128)S(1)}, bf16[1024,128]{1,0:T(8,128)(2,1)}, bf16[...) custom-call(s32[64]{0:T(128)} %pos_ref.5, bf16[64,2048]{1,0:T(8,128)(2,1)} %tok_ref.3, ...), custom_call_target="tpu_custom_call" | custom-call | tf_op jit(solution)/shard_map/pallas_call | solution.py:438
  40.8 0.0 copy-done.1
  40.8 0.0 copy-start
  40.8 18.5 %shard_map.148 = (f32[768,128]{1,0:T(8,128)S(1)}, f32[256,128]{1,0:T(8,128)S(1)}, bf16[4,2048,512]{2,1,0:T(8,128)(2,1)S(1)}, bf16[16,2048,128]{2,1,0:T(8,128)(2,1)S(1)}, bf16[16,2048,128]{2,1,0:T(8,128)(2,1)S(1)}) custom-call(s32[64]{0:T(128)S(1)} %copy-done.1, f32[1024,128]{1,0:T(8,128)S(1)} %get-tuple-element.19.q_ref, ...), custom_call_target="tpu_custom_call" | custom-call | tf_op jit(solution)/shard_map/pallas_call | solution.py:452
  59.4 0.0 copy-done
  59.4 7.3 %shard_map.149 = (bf16[64,2048]{1,0:T(8,128)(2,1)}, bf16[16,2048,128]{2,1,0:T(8,128)(2,1)S(1)}, bf16[16,2048,128]{2,1,0:T(8,128)(2,1)S(1)}, bf16[64,2048,128]{2,1,0:T(8,128)(2,1)}, bf16[64,2048,128]{2,1,0:T(8,128)(2,1)}) custom-call(s32[64]{0:T(128)S(1)} %copy-done.1, ...), custom_call_target="tpu_custom_call", output_to_operand_aliasing={{1}: (6, {}), {2}: (7, {}), {3}: (8, {}), {4}: (9, {})} | custom-call | tf_op jit(solution)/shard_map/pallas_call | solution.py:467
Async XLA Ops:
  0.6 40.2 %copy-start.1 = (s32[64]{0:T(128)S(1)}, s32[64]{0:T(128)}, u32[]{:S(2)}) copy-start(s32[64]{0:T(128)} %pos_ref.5) | copy-start | bytes 772
  40.8 18.5 %copy-start = (bf16[64,2048]{1,0:T(8,128)(2,1)S(1)}, bf16[64,2048]{1,0:T(8,128)(2,1)}, u32[]{:S(2)}) copy-start(bf16[64,2048]{1,0:T(8,128)(2,1)} %tok_ref.3) | copy-start | bytes 786436

commit v7 on v6

--- a/solution.py
+++ b/solution.py
@@ -29,9 +29,9 @@
 PART_E = OWN_E * HEADS + 8
 PART_L = OWN_L * HEADS + 8
 CHUNK = 512
-RING = 16
+RING = 24
 PAIRS = RING // 2
-LAG = 3
+LAG = 5
 COLS = 512
 CHUNKS = WIDTH // COLS
 
@@ -239,11 +239,11 @@
             copy.start()
         return carry
 
-    lax.fori_loop(0, 2, start_reads, 0)
-
     barrier = pltpu.get_barrier_semaphore()
     for m in range(1, RANKS):
         pl.semaphore_signal(barrier, inc=1, device_id={'sp': flip(me, m)}, device_id_type=MESH)
+    lax.fori_loop(0, 2, start_reads, 0)
+    key[...] = head_columns()
     pl.semaphore_wait(barrier, RANKS - 1)
     for m in range(RANKS - 1, 0, -1):
         early_copy(m).start()
@@ -251,7 +251,6 @@
     for c in range(CHUNKS):
         wo_copy(c).start()
     recv_e[0] = early_ref[me]
-    key[...] = head_columns()
 
     row16 = lax.broadcasted_iota(jnp.int32, (HEADS, 2 * KV), 0)
     col16 = lax.broadcasted_iota(jnp.int32, (HEADS, 2 * KV), 1)

time: 66.8 us -> 67.3 us (level)
  no operation moved by 1% of the time
where the time goes in v7:
time: 67.3 us; the launch traced here: 67.2 us
  Pallas kernels  66.5 us (99%)
  between operations  0.68 us (1%)
    pallas_call x1, Pallas kernels, device_step(): pl.pallas_call(early_kernel, out_shape=(space((RANKS, PART_E, DIM), F32),...  40.6 us
    pallas_call x1, Pallas kernels, device_step(): pl.pallas_call(late_kernel, out_shape=(space((EARLY * HEADS, DIM), F32),...  18.6 us
    pallas_call x1, Pallas kernels, device_step(): pl.pallas_call(store_kernel, out_shape=(sds((SEQS, WIDTH), BF16), space((...  7.34 us

profile of v7, /device:TPU:0, one launch (start us, length us, event | category | flops | bytes accessed | tf_op | source)
XLA Modules:
  0.0 67.2 jit_solution(8376195935853292060)
XLA Ops:
  0.6 0.0 copy-start.1
  0.6 40.6 %shard_map.147 = (f32[8,104,128]{2,1,0:T(8,128)S(1)}, f32[1024,128]{1,0:T(8,128)S(1)}, f32[1024,128]{1,0:T(8,128)S(1)}, bf16[1024,128]{1,0:T(8,128)(2,1)}, bf16[...) custom-call(s32[64]{0:T(128)} %pos_ref.5, bf16[64,2048]{1,0:T(8,128)(2,1)} %tok_ref.3, ...), custom_call_target="tpu_custom_call" | custom-call | tf_op jit(solution)/shard_map/pallas_call | solution.py:437
  41.3 0.0 copy-done.1
  41.3 0.0 copy-start
  41.3 18.6 %shard_map.148 = (f32[768,128]{1,0:T(8,128)S(1)}, f32[256,128]{1,0:T(8,128)S(1)}, bf16[4,2048,512]{2,1,0:T(8,128)(2,1)S(1)}, bf16[16,2048,128]{2,1,0:T(8,128)(2,1)S(1)}, bf16[16,2048,128]{2,1,0:T(8,128)(2,1)S(1)}) custom-call(s32[64]{0:T(128)S(1)} %copy-done.1, f32[1024,128]{1,0:T(8,128)S(1)} %get-tuple-element.19.q_ref, ...), custom_call_target="tpu_custom_call" | custom-call | tf_op jit(solution)/shard_map/pallas_call | solution.py:451
  59.9 0.0 copy-done
  59.9 7.3 %shard_map.149 = (bf16[64,2048]{1,0:T(8,128)(2,1)}, bf16[16,2048,128]{2,1,0:T(8,128)(2,1)S(1)}, bf16[16,2048,128]{2,1,0:T(8,128)(2,1)S(1)}, bf16[64,2048,128]{2,1,0:T(8,128)(2,1)}, bf16[64,2048,128]{2,1,0:T(8,128)(2,1)}) custom-call(s32[64]{0:T(128)S(1)} %copy-done.1, ...), custom_call_target="tpu_custom_call", output_to_operand_aliasing={{1}: (6, {}), {2}: (7, {}), {3}: (8, {}), {4}: (9, {})} | custom-call | tf_op jit(solution)/shard_map/pallas_call | solution.py:466
Async XLA Ops:
  0.6 40.7 %copy-start.1 = (s32[64]{0:T(128)S(1)}, s32[64]{0:T(128)}, u32[]{:S(2)}) copy-start(s32[64]{0:T(128)} %pos_ref.5) | copy-start | bytes 772
  41.3 18.6 %copy-start = (bf16[64,2048]{1,0:T(8,128)(2,1)S(1)}, bf16[64,2048]{1,0:T(8,128)(2,1)}, u32[]{:S(2)}) copy-start(bf16[64,2048]{1,0:T(8,128)(2,1)} %tok_ref.3) | copy-start | bytes 786436

commit v8 on v6

--- a/solution.py
+++ b/solution.py
@@ -248,8 +248,6 @@
     for m in range(RANKS - 1, 0, -1):
         early_copy(m).start()
     lax.fori_loop(2, LATE // 2, start_reads, 0)
-    for c in range(CHUNKS):
-        wo_copy(c).start()
     recv_e[0] = early_ref[me]
     key[...] = head_columns()
 
@@ -314,7 +312,10 @@
             acc = acc + w * recv[s, pl.ds(0, rows), :]
         return acc / total
 
-    def gather(own, out, gs, gr):
+    def gather(own, out, gs, gr, relayed):
+        direct = (6, 4, 2, 1) if relayed else (7, 6, 5, 4, 3, 2, 1)
+        through = (2, 4, 6) if relayed else ()
+        rest = (1, 3, 5, 7) if relayed else direct
         size = own.shape[0]
 
         def place(rank):
@@ -332,38 +333,42 @@
             return remote(own, place(src), gs.at[mask], gr.at[src], mask)
 
         def first():
-            for mask in (6, 4, 2, 1):
+            for mask in direct:
                 send(mask).start()
             out[pl.ds(pl.multiple_of(me * size, size), size), :] = own[...]
 
         def second():
-            for mask in (2, 4, 6):
+            for mask in through:
                 arrival(mask).wait_recv()
                 relay(mask).start()
 
         def last():
-            for mask in (1, 3, 5, 7):
+            for mask in rest:
                 arrival(mask).wait_recv()
-            for mask in (6, 4, 2, 1):
+            for mask in direct:
                 send(mask).wait_send()
-            for mask in (2, 4, 6):
+            for mask in through:
                 relay(mask).wait_send()
 
         return first, second, last
 
-    stages_e = gather(own_e, out_e, ges, ger)
-    stages_l = gather(own_l, out_l, gls, glr)
+    stages_e = gather(own_e, out_e, ges, ger, True)
+    stages_l = gather(own_l, out_l, gls, glr, False)
     lax.fori_loop(0, RANKS - 1, group, 0)
     for m in range(RANKS - 1, 0, -1):
         early_copy(m).wait()
     own_e[...] = combine(recv_e, OWN_E)
     stages_e[0]()
+    for c in range(CHUNKS // 2):
+        wo_copy(c).start()
     lax.fori_loop(RANKS - 1, RANKS, group, 0)
     recv_l[0] = late[0]
     for m in range(RANKS - 1, 0, -1):
         late_copy(m).wait()
     own_l[...] = combine(recv_l, OWN_L)
     stages_l[0]()
+    for c in range(CHUNKS // 2, CHUNKS):
+        wo_copy(c).start()
     stages_e[1]()
     stages_l[1]()
     for c in range(CHUNKS):

time: 66.8 us -> 66.8 us (level)
  no operation moved by 1% of the time
where the time goes in v8:
time: 66.8 us; the launch traced here: 66.7 us
  Pallas kernels  66 us (99%)
  between operations  0.68 us (1%)
    pallas_call x1, Pallas kernels, device_step(): pl.pallas_call(early_kernel, out_shape=(space((RANKS, PART_E, DIM), F32),...  40.2 us
    pallas_call x1, Pallas kernels, device_step(): pl.pallas_call(late_kernel, out_shape=(space((EARLY * HEADS, DIM), F32),...  18.5 us
    pallas_call x1, Pallas kernels, device_step(): pl.pallas_call(store_kernel, out_shape=(sds((SEQS, WIDTH), BF16), space((...  7.34 us

profile of v8, /device:TPU:0, one launch (start us, length us, event | category | flops | bytes accessed | tf_op | source)
XLA Modules:
  0.0 66.7 jit_solution(7426087704113986837)
XLA Ops:
  0.6 0.0 copy-start.1
  0.6 40.2 %shard_map.147 = (f32[8,104,128]{2,1,0:T(8,128)S(1)}, f32[1024,128]{1,0:T(8,128)S(1)}, f32[1024,128]{1,0:T(8,128)S(1)}, bf16[1024,128]{1,0:T(8,128)(2,1)}, bf16[...) custom-call(s32[64]{0:T(128)} %pos_ref.5, bf16[64,2048]{1,0:T(8,128)(2,1)} %tok_ref.3, ...), custom_call_target="tpu_custom_call" | custom-call | tf_op jit(solution)/shard_map/pallas_call | solution.py:443
  40.8 0.0 copy-done.1
  40.8 0.0 copy-start
  40.8 18.5 %shard_map.148 = (f32[768,128]{1,0:T(8,128)S(1)}, f32[256,128]{1,0:T(8,128)S(1)}, bf16[4,2048,512]{2,1,0:T(8,128)(2,1)S(1)}, bf16[16,2048,128]{2,1,0:T(8,128)(2,1)S(1)}, bf16[16,2048,128]{2,1,0:T(8,128)(2,1)S(1)}) custom-call(s32[64]{0:T(128)S(1)} %copy-done.1, f32[1024,128]{1,0:T(8,128)S(1)} %get-tuple-element.19.q_ref, ...), custom_call_target="tpu_custom_call" | custom-call | tf_op jit(solution)/shard_map/pallas_call | solution.py:457
  59.4 0.0 copy-done
  59.4 7.3 %shard_map.149 = (bf16[64,2048]{1,0:T(8,128)(2,1)}, bf16[16,2048,128]{2,1,0:T(8,128)(2,1)S(1)}, bf16[16,2048,128]{2,1,0:T(8,128)(2,1)S(1)}, bf16[64,2048,128]{2,1,0:T(8,128)(2,1)}, bf16[64,2048,128]{2,1,0:T(8,128)(2,1)}) custom-call(s32[64]{0:T(128)S(1)} %copy-done.1, ...), custom_call_target="tpu_custom_call", output_to_operand_aliasing={{1}: (6, {}), {2}: (7, {}), {3}: (8, {}), {4}: (9, {})} | custom-call | tf_op jit(solution)/shard_map/pallas_call | solution.py:472
Async XLA Ops:
  0.6 40.2 %copy-start.1 = (s32[64]{0:T(128)S(1)}, s32[64]{0:T(128)}, u32[]{:S(2)}) copy-start(s32[64]{0:T(128)} %pos_ref.5) | copy-start | bytes 772
  40.8 18.6 %copy-start = (bf16[64,2048]{1,0:T(8,128)(2,1)S(1)}, bf16[64,2048]{1,0:T(8,128)(2,1)}, u32[]{:S(2)}) copy-start(bf16[64,2048]{1,0:T(8,128)(2,1)} %tok_ref.3) | copy-start | bytes 786436
